TPU v7x, 32 devices: a whole 2x2x4 slice. The times are simulated.
32 devices in a mesh: mom: 4 (over y, x), en: 8 (over z, core).
Axes of the slice: x: 2, y: 2, z: 4, core: 2. Of those that a mesh axis runs over, the one named last changes fastest.
Arguments:
- green_blocks: float32 [12, 8, 2, 512, 512], P('mom', 'en'), may hold values from -6 to 6
- transfer_index: int32 [12, 12], P('mom'), may hold values from 0 to 8
- photon_shift: int32 [12], P('mom'), may hold values from 1 to 2
- photon_occupancy: float32 [1], replicated, may hold values from 0.3 to 3
- coupling: bfloat16 [9, 512, 512], replicated, may hold values from -0.25 to 0.25
Outputs:
- self_energy: float32 [12, 8, 2, 512, 512], P('mom', 'en')
All inputs are finite; a program needn't handle non-finite values.
Results may differ from a plain program's by a relative error of at most 0.0057.
Values may be sent and summed in bfloat16 or wider, within the bound.
No kernel may reach another device: no remote copies, remote signals or barrier semaphores. Data moves between devices by JAX's collectives and lax.ppermute only.
A program may use at most 192 MiB of HBM per device.

v0:
```python
import jax
import jax.numpy as jnp
from jax import lax
from jax.sharding import PartitionSpec as P


def from_behind(value, axis, steps):
    count = lax.axis_size(axis)
    first, last = (max(0, -steps), min(count, count - steps))
    return lax.ppermute(value, axis, [(source, source + steps) for source in range(first, last)])


def body(green_blocks, transfer_index, photon_shift, photon_occupancy, coupling):
    rounded = green_blocks.astype(jnp.bfloat16)
    near_mask = (photon_shift == 1)[:, None, None, None, None]
    occupy = photon_occupancy[0]
    local_moms = rounded.shape[0]
    orbitals = rounded.shape[3]
    momenta = transfer_index.shape[1]
    classes = coupling.shape[0]
    nearby = {}
    further = {}
    for offset in (1, -1):
        nearby[offset] = from_behind(rounded, "en", offset)
    for offset in (1, -1):
        further[offset] = from_behind(nearby[offset], "en", offset)
    below_rim = jnp.where(near_mask, nearby[1], further[1])
    above_rim = jnp.where(near_mask, nearby[-1], further[-1])
    mixed = (
        occupy * below_rim.astype(jnp.float32) + (occupy + 1.0) * above_rim.astype(jnp.float32)
    ).astype(jnp.bfloat16)
    flat = mixed.reshape(local_moms, -1)
    selector = (
        transfer_index[:, None, :] == jnp.arange(classes, dtype=jnp.int32)[None, :, None]
    ).astype(jnp.bfloat16)
    selector = selector.reshape(local_moms * classes, momenta)
    whole = lax.all_gather(flat, "mom", axis=0, tiled=True)
    bins = jnp.dot(selector, whole, preferred_element_type=jnp.float32)
    bins = bins.astype(jnp.bfloat16).reshape(local_moms, classes, 2, orbitals, orbitals)
    left = jnp.einsum(
        "qxy,kqcyz->kqcxz", coupling, bins, preferred_element_type=jnp.float32
    ).astype(jnp.bfloat16)
    result = jnp.einsum("kqcxy,qzy->kcxz", left, coupling, preferred_element_type=jnp.float32)
    result = result / momenta
    return result[:, None]


def solution(mesh):
    placed = (P("mom", "en", None, None, None), P("mom", None), P("mom"), P(), P())
    return jax.shard_map(
        body,
        mesh=mesh,
        in_specs=placed,
        out_specs=P("mom", "en", None, None, None),
        check_vma=False,
    )
```

profile of v0, /device:TPU:0, one launch (start us, length us, event | category | flops | bytes accessed | tf_op | source)
XLA Modules:
  0.0 399.7 jit_solution(14671406999848466934)
XLA Ops:
  6.5 0.0 copy-start.2
  6.5 0.0 all-gather.3.cloned.1.call-start
  6.5 3.2 convert_element_type.22
  9.7 1.3 collective-permute-start.2
  11.0 4.7 %collective-permute-start = (bf16[3,1,2,512,512]{4,3,2,1,0:T(8,128)(2,1)S(1)}, bf16[3,1,2,512,512]{4,3,2,1,0:T(8,128)(2,1)}, u32[]{:S(2)}, u32[]{:S(2)}) collective-permute-start(bf16[3,1,2,512,512]{4,3,2,1,0:T(8,128)(2,1)S(1)} %convert_element_type.22), channel_id=1, source_target_pairs={{0,1},{1,2},{2,3},{3,4},{4,5},{5,6},{6,7},{8,9},{9,10},{10,11},{11... | collective-permute-start | bytes 9437192 | tf_op jit(solution)/shard_map/ppermute | solution.py:10
  15.8 1.5 collective-permute-done.2
  17.3 0.0 copy-start
  17.3 1.3 collective-permute-start.3
  18.6 0.9 collective-permute-done
  19.5 35.8 %collective-permute-start.1 = (bf16[3,1,2,512,512]{4,3,2,1,0:T(8,128)(2,1)}, bf16[3,1,2,512,512]{4,3,2,1,0:T(8,128)(2,1)}, u32[]{:S(2)}, u32[]{:S(2)}) collective-permute-start(bf16[3,1,2,512,512]{4,3,2,1,0:T(8,128)(2,1)} %collective-permute-done), channel_id=1, source_target_pairs={{0,1},{1,2},{2,3},{3,4},{4,5},{5,6},{6,7},{8,9},{9,10},{10,11},{11... | collective-permute-start | bytes 9437192 | tf_op jit(solution)/shard_map/ppermute | solution.py:10
  56.0 0.0 copy-done.2
  56.0 1.0 collective-permute-done.3
  56.9 2.3 collective-permute-done.1
  59.2 0.0 copy-done
  59.2 6.7 %add_convert_fusion = bf16[3,1,2,512,512]{4,3,2,1,0:T(8,128)(2,1)S(1)} fusion(bf16[3,1,2,512,512]{4,3,2,1,0:T(8,128)(2,1)} %copy-done, bf16[3,1,2,512,512]{4,3,2,1,0:T(8,128)(2,1)} %collective-permute-done.3, f32[]{:T(128)S(6)} %add.6, bf16[3,1,2,512,512]{4,3,2,1,0:T(8,128)(2,1)} %collective-permute-done, ...), kind=kLoop, calls=%fused_computation.8 | loop fusion | flops 12582912 | bytes 15728651 | tf_op jit(solution)/shard_map/convert_element_type | solution.py:31
  66.0 0.0 copy-start.1
  66.0 4.1 %reshape.15 = bf16[1,3,524288]{2,1,0:T(4,128)(2,1)} reshape(bf16[3,1,2,512,512]{4,3,2,1,0:T(8,128)(2,1)S(1)} %add_convert_fusion) | data formatting | bytes 6291456
  70.1 0.0 all-gather.3.cloned.1.call-update
  70.1 0.1 eq.26
  70.2 0.0 copy-done.1
  70.2 0.1 copy.9
  70.3 0.1 eq.23
  70.4 0.1 eq.24
  70.5 190.2 %all-gather.3.cloned.1.call-done = bf16[4,3,524288]{2,1,0:T(4,128)(2,1)} async-done(((bf16[1,3,524288]{2,1,0:T(4,128)(2,1)}), bf16[4,3,524288]{2,1,0:T(4,128)(2,1)}) %all-gather.3.cloned.1.call-update) | async-done | bytes 12582928 | tf_op jit(solution)/shard_map/all_gather | solution.py:37
  260.6 28.8 %reshape.16 = bf16[12,524288]{1,0:T(8,128)(2,1)} reshape(bf16[4,3,524288]{2,1,0:T(4,128)(2,1)} %all-gather.3.cloned.1.call-done) | data formatting | bytes 25165824
  289.4 19.5 %convolution_convert_fusion = bf16[27,524288]{1,0:T(8,128)(2,1)} fusion(bf16[12,524288]{1,0:T(8,128)(2,1)} %reshape.16, s32[27,12]{0,1:T(8,128)S(1)} %eq.24, s32[27]{0:T(128)S(1)} %eq.26), kind=kOutput, calls=%fused_computation | convolution fusion | flops 353894720 | bytes 40895868 | tf_op jit(solution)/shard_map/dot_general | solution.py:38
  308.9 22.7 %copy.18 = bf16[4,8,1024,512]{3,2,1,0:T(8,128)(2,1)} copy(bf16[4,8,1024,512]{3,1,2,0:T(8,128)(2,1)} %bitcast.36) | data formatting | bytes 67108864
  331.6 19.7 %slice = bf16[27,1024,512]{2,1,0:T(8,128)(2,1)} slice(bf16[32,1024,512]{2,1,0:T(8,128)(2,1)} %bitcast.37), slice={[0:27], [0:1024], [0:512]} | slice | bytes 56623104
  351.3 41.6 %fusion.9 = f32[3,1,2,512,512]{4,3,2,1,0:T(8,128)} fusion(bf16[9,512,512]{2,1,0:T(8,128)(2,1)} %param.9, bf16[3,9,2,512,512]{4,3,2,1,0:T(8,128)(2,1)} %bitcast.38), kind=kOutput, calls=%fused_computation.7 | convolution fusion | flops 29006757888 | bytes 39321600 | tf_op jit(solution)/shard_map/kqcxy,qzy->kcxz/dot_general | solution.py:43
  (2 shorter events, 0.0 us)
Async XLA Ops:
  6.5 49.4 %copy-start.2 = (s32[3]{0:T(128)S(1)}, s32[3]{0:T(128)}, u32[]{:S(2)}) copy-start(s32[3]{0:T(128)} %param.7) | copy-start | bytes 40
  6.5 254.1 %all-gather.3.cloned.1.call-start = ((), (), s32[]{:S(2)}) async-start(), calls=%async_computation | async-start | bytes 20971520 | tf_op jit(solution)/shard_map/all_gather | solution.py:37
  9.7 7.6 %collective-permute-start.2 = (bf16[3,1,2,512,512]{4,3,2,1,0:T(8,128)(2,1)S(1)}, bf16[3,1,2,512,512]{4,3,2,1,0:T(8,128)(2,1)S(1)}, u32[]{:S(2)}, u32[]{:S(2)}) collective-permute-start(bf16[3,1,2,512,512]{4,3,2,1,0:T(8,128)(2,1)S(1)} %convert_element_type.22), channel_id=1, source_target_pairs={{1,0},{2,1},{3,2},{4,3},{5,4},{6,5},{7,6},{9,8},{10,9},{11,10},{12... | collective-permute-start | bytes 9437192 | tf_op jit(solution)/shard_map/ppermute | solution.py:10
  11.0 8.4 %collective-permute-start = (bf16[3,1,2,512,512]{4,3,2,1,0:T(8,128)(2,1)S(1)}, bf16[3,1,2,512,512]{4,3,2,1,0:T(8,128)(2,1)}, u32[]{:S(2)}, u32[]{:S(2)}) collective-permute-start(bf16[3,1,2,512,512]{4,3,2,1,0:T(8,128)(2,1)S(1)} %convert_element_type.22), channel_id=1, source_target_pairs={{0,1},{1,2},{2,3},{3,4},{4,5},{5,6},{6,7},{8,9},{9,10},{10,11},{11... | collective-permute-start | bytes 9437192 | tf_op jit(solution)/shard_map/ppermute | solution.py:10
  17.3 41.9 %copy-start = (bf16[3,1,2,512,512]{4,3,2,1,0:T(8,128)(2,1)}, bf16[3,1,2,512,512]{4,3,2,1,0:T(8,128)(2,1)S(1)}, u32[]{:S(2)}) copy-start(bf16[3,1,2,512,512]{4,3,2,1,0:T(8,128)(2,1)S(1)} %collective-permute-done.2) | copy-start | bytes 9437188
  17.3 39.6 %collective-permute-start.3 = (bf16[3,1,2,512,512]{4,3,2,1,0:T(8,128)(2,1)S(1)}, bf16[3,1,2,512,512]{4,3,2,1,0:T(8,128)(2,1)}, u32[]{:S(2)}, u32[]{:S(2)}) collective-permute-start(bf16[3,1,2,512,512]{4,3,2,1,0:T(8,128)(2,1)S(1)} %collective-permute-done.2), channel_id=1, source_target_pairs={{1,0},{2,1},{3,2},{4,3},{5,4},{6,5},{7,6},{9,8},{10,9},{11,10},{12... | collective-permute-start | bytes 9437192 | tf_op jit(solution)/shard_map/ppermute | solution.py:10
  19.5 39.7 %collective-permute-start.1 = (bf16[3,1,2,512,512]{4,3,2,1,0:T(8,128)(2,1)}, bf16[3,1,2,512,512]{4,3,2,1,0:T(8,128)(2,1)}, u32[]{:S(2)}, u32[]{:S(2)}) collective-permute-start(bf16[3,1,2,512,512]{4,3,2,1,0:T(8,128)(2,1)} %collective-permute-done), channel_id=1, source_target_pairs={{0,1},{1,2},{2,3},{3,4},{4,5},{5,6},{6,7},{8,9},{9,10},{10,11},{11... | collective-permute-start | bytes 9437192 | tf_op jit(solution)/shard_map/ppermute | solution.py:10
  66.0 4.2 %copy-start.1 = (s32[3,12]{1,0:T(4,128)S(1)}, s32[3,12]{1,0:T(4,128)}, u32[]{:S(2)}) copy-start(s32[3,12]{1,0:T(4,128)} %param.6) | copy-start | bytes 436
Sparse Core Ops, SparseCore 0:
  70.2 190.3 all-gather.2
where the time goes:
time: 400 us
  waiting for transfers between devices  196 us (49%)
  local copies, waits for them, and re-layouts  75.6 us (19%)
  matrix products  61.1 us (15%)
  starting transfers between devices  43.1 us (11%)
  between operations  14.1 us (4%)
  other arithmetic  9.93 us (2%)
    all_gather x1, waiting for transfers between devices, body(): whole = lax.all_gather(flat, 'mom', axis=0, tiled=True)  190 us
    unnamed x11, local copies, waits for them, and re-layouts  75.4 us
    ppermute x4, starting transfers between devices, from_behind(): lax.ppermute(value, axis, [(source, source + steps) for source in range(f...  43.1 us
    dot_general x1, matrix products, body(): jnp.einsum('kqcxy,qzy->kcxz', left, coupling, preferred_element_type=jnp....  41.6 us
    dot_general x1, matrix products, body(): bins = jnp.dot(selector, whole, preferred_element_type=jnp.float32)  19.5 us
  transfers between devices with their start and end apart: 5, of which 5 were waited for; matrix products, arithmetic and copies ran while one was open for 0% of the time, Pallas kernels for 0%

commit v1 on v0

v1 whole, which is shorter than its diff:
```python
import functools

import jax
import jax.numpy as jnp
from jax import lax
from jax.experimental import pallas as pl
from jax.experimental.pallas import tpu as pltpu
from jax.sharding import PartitionSpec as P


MEMBERS = 4
FIELDS = 8
SIZES = (4, 2, 1)
MIB = 1 << 20
LAST_ROWS = (((1,), (1,)), ((), ()))


def pieces_of(local):
    return [1] * (2 * local - 1) + [2]


def settle(near, occupancy, place, weights):
    local = len(near)
    occupy = occupancy[0]
    even, has_toward, has_away = place[0] == 1, place[1] == 1, place[2] == 1
    weights[0] = jnp.where(has_toward, jnp.where(even, occupy, occupy + 1.0), 0.0)
    heavy = jnp.where(even, occupy + 1.0, occupy)
    for k in range(local):
        weights[1 + k] = jnp.where(near[k], heavy, 0.0)
        weights[1 + local + k] = jnp.where(near[k] | jnp.logical_not(has_away), 0.0, heavy)


def plan_kernel(sizes, own_ref, partner_ref, occupancy, sides, place_ref, table, weights, count, member, filled):
    local, momenta, classes, bits, calls = sizes
    ways = 1 << bits
    slots = 2 * local * ways
    bins = 2 * local * classes
    room = 2 * local * momenta
    near = [lax.div(partner_ref[k, 0], classes) == 1 for k in range(local)]
    settle(near, occupancy, sides, weights)

    for index in range(bins):
        count[index] = 0
    for call in range(calls):
        filled[call] = 0
        table[call] = 0

    def sort_slot(slot, _):
        stage = lax.div(slot, ways)
        way = lax.rem(slot, ways)
        home = place_ref[0]
        for bit in range(bits):
            home = home ^ jnp.where((way >> bit) & 1 == 1, place_ref[2 + bit], 0)
        home = home ^ jnp.where(stage < local, 0, place_ref[1])
        momentum = home * local + lax.rem(stage, local)
        for k in range(2 * local):
            of_k = partner_ref[k, momentum] if k < local else own_ref[k - local, momentum]
            of_k = lax.rem(of_k, classes)
            index = k * classes + of_k
            have = count[index]
            member[index * slots + have] = slot
            count[index] = have + 1
        return 0

    lax.fori_loop(0, slots, sort_slot, 0)

    for k in range(2 * local):

        def one_bin(q, _):
            index = k * classes + q
            have = count[index]

            def one_job(j, _):
                first = index * slots + j * MEMBERS
                upto = jnp.minimum(MEMBERS, have - j * MEMBERS)
                stage = lax.div(member[first + upto - 1], ways)
                last = 2 * local - 1
                call = jnp.where(stage == last, last + 1 + min(k, local), stage)
                if k >= local:
                    call = jnp.where(stage == last - 1, last, call)
                place = filled[call]
                filled[call] = place + 1
                table[call] = place + 1
                at = calls + (call * room + place) * FIELDS
                table[at] = k
                table[at + 1] = q
                for i in range(MEMBERS):
                    table[at + 2 + i] = jnp.where(i < upto, member[first + i], slots)
                return 0

            return lax.fori_loop(0, lax.div(have + MEMBERS - 1, MEMBERS), one_job, 0)

        lax.fori_loop(0, classes, one_bin, 0)


def convert_first_kernel(part_ref, block, out):
    out[0] = block[0, 0].astype(out.dtype)


def convert_kernel(local, part_ref, shift, occupancy, sides, block, *outs):
    step = pl.program_id(0)
    low = outs[0].dtype
    weights, flags = outs[-2:]

    @pl.when(step == 0)
    def _():
        near = [shift[k] == 1 for k in range(local)]
        settle(near, occupancy, sides, weights)
        for k in range(local):
            flags[k] = jnp.where(near[k], 1, 0)

    for k in range(1, local):

        @pl.when(step == k)
        def _():
            outs[k - 1][0] = block[0, part_ref[0]].astype(low)

    outs[local - 1][step] = block[0, part_ref[1]].astype(low)
    outs[local][step] = block[0, part_ref[2]].astype(low)
    outs[local][local + step] = block[0, part_ref[3]].astype(low)


def choose_kernel(local, flags, mate, *refs):
    own, others, outs = refs[:local], refs[local], list(refs[local + 1 :])
    for k, cuts in enumerate(pieces_of(local)):
        rows = mate.shape[1] // cuts
        given, at = (own[k], 0) if k < local else (others, k - local)
        near = flags[k % local] == 1
        for top in range(0, mate.shape[1], rows):
            out = outs.pop(0)

            @pl.when(near)
            def _():
                out[0] = mate[k, top : top + rows]

            @pl.when(jnp.logical_not(near))
            def _():
                out[0] = given[at, top : top + rows]


def mix_kernel(k, local, weights, came, chosen, gone, out):
    wide = jnp.float32
    out[...] = (
        weights[0] * came[...].astype(wide)
        + (
            weights[1 + k] * chosen[...].astype(wide)
            + weights[1 + local + k] * gone[...].astype(wide)
        )
    ).astype(out.dtype)


def run_jobs(call, calls, table, coupling, blocks, total, wide=False):
    header = calls + call * ((table.shape[0] - calls) // calls)

    def step(i, _, first, jobs):
        for u in range(jobs):
            at = header + (first + i * jobs + u) * FIELDS
            k, q = table[at], table[at + 1]
            summed = blocks[table[at + 2]].astype(jnp.float32)
            for j in range(1, MEMBERS):
                summed = summed + blocks[table[at + 2 + j]].astype(jnp.float32)
            weight = coupling[q]
            left = jnp.dot(weight, summed.astype(blocks.dtype), preferred_element_type=jnp.float32)
            total[k] += lax.dot_general(
                left.astype(blocks.dtype), weight, LAST_ROWS, preferred_element_type=jnp.float32
            )
        return 0

    done, jobs = 0, table[call]
    for size in SIZES[0 if wide else 1 :]:
        count = lax.div(jobs - done, size)
        lax.fori_loop(0, count, functools.partial(step, first=done, jobs=size), 0)
        done = done + count * size


def stage_kernel(call, calls, base, ways, arrived, sends, scale, table, coupling, *refs):
    parts = refs[:arrived]
    first_call = call == 0
    refs = refs[arrived:] if first_call else refs[arrived + 2 :]
    blocks, total = refs[:2]
    send = refs[2] if len(refs) > 2 else None
    slots = blocks.shape[0] - 1
    if first_call:
        blocks[slots] = jnp.zeros(blocks.shape[1:], blocks.dtype)
        total[...] = jnp.zeros(total.shape, total.dtype)
    for way in range(ways if arrived else 0):
        top = 0
        for part in parts[way * arrived // ways : (way + 1) * arrived // ways]:
            rows = part.shape[1]
            blocks[base + way, top : top + rows] = part[0]
            top += rows
    run_jobs(call, calls, table, coupling, blocks, total)
    if send is not None:
        for i, k in enumerate(sends):
            send[i] = (total[k] * scale).astype(send.dtype)


def finish_kernel(call, calls, scale, table, part_ref, coupling, blocks, total_in, total, out, ready, done):
    run_jobs(call, calls, table, coupling, blocks, total, wide=True)
    local = ready.shape[0]
    copies = []
    for k in range(local):
        ready[k] = total[local + k] * scale
        copies.append(pltpu.make_async_copy(ready.at[k], out.at[k, 0, part_ref[0]], done.at[k]))
        copies[k].start()
    for copy in copies:
        copy.wait()


def write_other_kernel(at, part_ref, *refs):
    parts, (out, ready, done) = refs[:-4], refs[-3:]
    copies = []
    for k, part in enumerate(parts):
        ready[k] = part[0].astype(ready.dtype)
        place = out.at[at + k, 0, part_ref[0]]
        copies.append(pltpu.make_async_copy(ready.at[k], place, done.at[k]))
        copies[k].start()
    for copy in copies:
        copy.wait()


def solution(mesh):
    moms, energies = mesh.shape["mom"], mesh.shape["en"]
    bits = moms.bit_length() - 2
    top = moms // 2
    both = ("mom", "en")

    def move(value, target):
        pairs = []
        for m in range(moms):
            for e in range(energies):
                to_m, to_e = target(m, e)
                if not 0 <= to_e < energies:
                    to_m, to_e = m, e ^ 1
                pairs.append((m * energies + e, to_m * energies + to_e))
        return lax.ppermute(value, both, pairs)

    def away(m, e):
        return m, e + (2 if e % 2 else -2)

    def toward(m, e):
        return m, e + (-2 if e % 2 else 2)

    def core_mate(m, e):
        return m, e ^ 1

    def partner(m, e):
        return m ^ (top if e % 2 else 1), e

    def gather_bit(bit):
        return lambda m, e: (m ^ ((1 << bit) if e % 2 else (2 << bit)), e)

    def body(green_blocks, transfer_index, photon_shift, photon_occupancy, coupling):
        local, _, parts, orbitals, _ = green_blocks.shape
        momenta = transfer_index.shape[1]
        classes = coupling.shape[0]
        ways = 1 << bits
        slots = 2 * local * ways
        last = 2 * local - 1
        calls = last + local + 2
        low = jnp.bfloat16
        scale = 1.0 / momenta
        m, e = lax.axis_index("mom"), lax.axis_index("en")
        even = e % 2 == 0
        bit_of = (m & 1, (m // top) & 1)
        mine = jnp.where(even, bit_of[0], bit_of[1])
        mates = jnp.where(even, bit_of[1], bit_of[0])
        flat = green_blocks.reshape(local, parts, orbitals, orbitals)
        block_shape = (orbitals, orbitals)
        smem = pl.BlockSpec(memory_space=pltpu.SMEM)
        vmem = pl.BlockSpec(memory_space=pltpu.VMEM)
        product = 4 * orbitals**3
        pieces = pieces_of(local)

        def kernel(act, *args, flops=1 << 20, vmem_mib=8, **more):
            return pl.pallas_call(
                act,
                compiler_params=pltpu.CompilerParams(vmem_limit_bytes=vmem_mib * MIB),
                cost_estimate=pl.CostEstimate(flops=flops, bytes_accessed=MIB, transcendentals=0),
                **more,
            )(*args)

        def send(value, target):
            came = move(value, target)
            if value.dtype != low:
                return came
            return pltpu.with_memory_space_constraint(came, pltpu.VMEM)

        place = jnp.stack(
            [m, jnp.where(even, 1, top)]
            + [jnp.where(even, 2 << bit, 1 << bit) for bit in range(bits)]
        ).astype(jnp.int32)
        has_below, has_above = e >= 2, e + 2 < energies
        sides = jnp.stack(
            [even, jnp.where(even, has_below, has_above), jnp.where(even, has_above, has_below)]
        ).astype(jnp.int32)
        which = jnp.stack([mine, 1 - mine, mates, 1 - mates]).astype(jnp.int32)
        place, sides, which = lax.optimization_barrier((place, sides, which))
        packed = transfer_index + classes * photon_shift[:, None]
        partner_index = send(packed, partner)

        flat = pltpu.with_memory_space_constraint(flat, pltpu.HBM)
        near_unit = pltpu.VMEM((1, *block_shape), low)
        near_units = pltpu.VMEM((local, *block_shape), low)
        weight_count = pltpu.SMEM((1 + 2 * local,), jnp.float32)
        first = kernel(
            convert_first_kernel,
            which,
            flat,
            grid_spec=pltpu.PrefetchScalarGridSpec(
                num_scalar_prefetch=1,
                grid=(1,),
                in_specs=[pl.BlockSpec((1, 1, *block_shape), lambda i, p: (0, p[0], 0, 0))],
                out_specs=vmem,
            ),
            out_shape=near_unit,
        )
        *rounded, own_weights, flags = kernel(
            functools.partial(convert_kernel, local),
            which,
            photon_shift,
            photon_occupancy,
            sides,
            flat,
            grid_spec=pltpu.PrefetchScalarGridSpec(
                num_scalar_prefetch=1,
                grid=(local,),
                in_specs=[smem] * 3
                + [pl.BlockSpec((1, parts, *block_shape), lambda i, p: (i, 0, 0, 0))],
                out_specs=[vmem] * (local + 1) + [smem] * 2,
            ),
            out_shape=[near_unit] * (local - 1)
            + [near_units, pltpu.VMEM((2 * local, *block_shape), low)]
            + [weight_count, pltpu.SMEM((local,), jnp.int32)],
        )
        own, (others, mates_blocks) = [first, *rounded[: local - 1]], rounded[local - 1 :]
        mate = send(mates_blocks, core_mate)
        ready = kernel(
            functools.partial(choose_kernel, local),
            flags,
            mate,
            *own,
            others,
            in_specs=[smem] + [vmem] * (2 + local),
            out_specs=[vmem] * sum(pieces),
            out_shape=[
                pltpu.VMEM((1, orbitals // n, orbitals), low) for n in pieces for _ in range(n)
            ],
        )
        ready = list(ready)
        ready = [[ready.pop(0) for _ in range(n)] for n in pieces]

        def sends(values, target):
            return [send(value, target) for value in values]

        gone = [sends([own[k]], away) for k in range(local)]
        chosen = ready[:local]
        chosen += [sends(ready[k], partner) for k in range(local, 2 * local)]
        gone += [sends(chosen[k], away) for k in range(local, 2 * local)]
        came = [sends(value, toward) for value in chosen]
        bins = 2 * local * classes
        room = calls + calls * 2 * local * momenta * FIELDS
        table, partner_weights = kernel(
            functools.partial(plan_kernel, (local, momenta, classes, bits, calls)),
            packed,
            partner_index,
            photon_occupancy,
            sides,
            place,
            in_specs=[smem] * 5,
            out_specs=[smem] * 2,
            out_shape=[pltpu.SMEM((room,), jnp.int32), weight_count],
            scratch_shapes=[
                pltpu.SMEM((bins,), jnp.int32),
                pltpu.SMEM((bins * slots,), jnp.int32),
                pltpu.SMEM((calls,), jnp.int32),
            ],
        )

        stages = [
            [
                kernel(
                    functools.partial(mix_kernel, k % local, local),
                    own_weights if k < local else partner_weights,
                    came[k][i],
                    chosen[k][i],
                    gone[k][i],
                    in_specs=[smem] + [vmem] * 3,
                    out_specs=vmem,
                    out_shape=pltpu.VMEM(came[k][i].shape, low),
                )
                for i in range(pieces[k])
            ]
            for k in range(2 * local)
        ]

        weights = pltpu.with_memory_space_constraint(coupling, pltpu.VMEM)
        out_state = [
            pltpu.VMEM((slots + 1, *block_shape), low),
            pltpu.VMEM((2 * local, *block_shape), jnp.float32),
        ]

        def stage(call, arrived, state, sends, jobs, base=0):
            given = [] if state is None else list(state)
            result = kernel(
                functools.partial(stage_kernel, call, calls, base, ways, len(arrived), sends, scale),
                table,
                weights,
                *arrived,
                *given,
                flops=jobs * product,
                vmem_mib=12,
                in_specs=[smem, vmem] + [vmem] * (len(arrived) + len(given)),
                out_specs=[vmem] * (2 + bool(sends)),
                out_shape=out_state + [pltpu.VMEM((len(sends), *block_shape), low)] * bool(sends),
                input_output_aliases={2 + len(arrived) + i: i for i in range(len(given))},
            )
            return result[:2], result[2:]

        state = None
        got = []
        for call, held in enumerate(stages):
            arrived = [held]
            for bit in range(bits):
                for values in list(arrived):
                    arrived.append(sends(values, gather_bit(bit)))
            arrived = [piece for values in arrived for piece in values]
            sends_now = [0] if call == last else []
            state, sent = stage(call + (call == last), arrived, state, sends_now, 5, call * ways)
        got = []
        for k in range(local):
            if k:
                state, sent = stage(last + 1 + k, [], state, [k], 2)
            got.append(send(sent[0], partner))
        state, _ = stage(last, [], state, [], 5)

        hbm = pl.BlockSpec(memory_space=pltpu.HBM)
        out_shape = jax.ShapeDtypeStruct(green_blocks.shape, jnp.float32)
        staging = [
            pltpu.VMEM((local, *block_shape), jnp.float32),
            pltpu.SemaphoreType.DMA((local,)),
        ]
        _, result = kernel(
            functools.partial(finish_kernel, last + 1 + local, calls, scale),
            table,
            mine.reshape(1),
            weights,
            *state,
            vmem_mib=14,
            in_specs=[smem] * 2 + [vmem] * 3,
            out_specs=[vmem, hbm],
            out_shape=[out_state[1], out_shape],
            input_output_aliases={4: 0},
            scratch_shapes=staging,
        )
        for name, values in (("early", got[:-1]), ("last", got[-1:])):
            result = kernel(
                functools.partial(write_other_kernel, 0 if name == "early" else local - 1),
                (1 - mine).reshape(1),
                *values,
                result,
                in_specs=[smem] + [vmem] * len(values) + [hbm],
                out_specs=hbm,
                out_shape=out_shape,
                input_output_aliases={1 + len(values): 0},
                scratch_shapes=staging,
            )
        return result

    placed = (P("mom", "en", None, None, None), P("mom", None), P("mom"), P(), P())

    return jax.shard_map(
        body,
        mesh=mesh,
        in_specs=placed,
        out_specs=P("mom", "en", None, None, None),
        check_vma=False,
    )
```

time: 400 us -> 138 us (0.34)
  waiting for transfers between devices: 196 us -> 53.6 us
  local copies, waits for them, and re-layouts: 75.6 us -> 0.67 us
  matrix products: 61.1 us -> 0 us
  Pallas kernels: 0 us -> 45.3 us
  between operations: 14.1 us -> 1.14 us
  other arithmetic: 9.93 us -> 0.3 us
  starting transfers between devices: 43.1 us -> 35.5 us
    all_gather x1 -> x0, waiting for transfers between devices: 190 us -> none  [body(): whole = lax.all_gather(flat, 'mom', axis=0, tiled=True)]
    unnamed x11 -> x10, local copies, waits for them, and re-layouts: 75.4 us -> 0.67 us
    dot_general x2 -> x0, matrix products: 61.1 us -> none  [the longest x1 41.6 us: body(): jnp.einsum('kqcxy,qzy->kcxz', left, coupling, preferred_element_type=jnp....]
    ppermute x4 -> x30, waiting for transfers between devices: 5.65 us -> 53.6 us  [move(): return lax.ppermute(value, both, pairs)]
    pallas_call x0 -> x23, Pallas kernels: none -> 45.3 us  [kernel(): pl.pallas_call(act, compiler_params=pltpu.CompilerParams(vmem_limit_bytes...]
    convert_element_type x2 -> x1, other arithmetic: 9.92 us -> 0.08 us  [body(): sides = jnp.stack([even, jnp.where(even, has_below, has_above), jnp.where...]
    ppermute x4 -> x30, starting transfers between devices: 43.1 us -> 35.5 us  [move(): return lax.ppermute(value, both, pairs)]
  transfers between devices with their start and end apart: 5 -> 30, of which waited for: 5 -> 11; matrix products, arithmetic and copies ran while one was open for 0% -> 0% of each run, Pallas kernels for 0% -> 27%
where the time goes in v1:
time: 138 us; the launch traced here: 137 us
  waiting for transfers between devices  53.6 us (39%)
  Pallas kernels  45.3 us (33%)
  starting transfers between devices  35.5 us (26%)
    ppermute x30, waiting for transfers between devices, move(): return lax.ppermute(value, both, pairs)  53.6 us
    pallas_call x23, Pallas kernels, kernel(): pl.pallas_call(act, compiler_params=pltpu.CompilerParams(vmem_limit_bytes...  45.3 us
    ppermute x30, starting transfers between devices, move(): return lax.ppermute(value, both, pairs)  35.5 us
  transfers between devices with their start and end apart: 30, of which 11 were waited for; matrix products, arithmetic and copies ran while one was open for 0% of the time, Pallas kernels for 27%

profile of v1, /device:TPU:0, one launch (start us, length us, event | category | flops | bytes accessed | tf_op | source)
XLA Modules:
  0.0 136.6 jit_solution(17393183020590632325)
XLA Ops:
  0.9 0.6 copy-done
  1.5 4.3 %shard_map.56 = (bf16[1,512,512]{2,1,0:T(8,128)(2,1)S(1)}, bf16[1,512,512]{2,1,0:T(8,128)(2,1)S(1)}, bf16[3,512,512]{2,1,0:T(8,128)(2,1)S(1)}, bf16[6,512,512]{2...) custom-call(s32[4]{0:T(128)S(1)} %pad_add_fusion.1.part_ref, s32[3]{0:T(128)S(1)} %copy-done, f32[1]{0:T(128)S(6)} %copy.44.occupancy, ...), custom_call_target="tpu_custom_call" | custom-call | flops 1048576 | bytes 1048576 | tf_op jit(solution)/shard_map/pallas_call | solution.py:276
  5.9 0.6 collective-permute-start.1
  6.4 1.8 %shard_map.57.refs_0_ = bf16[1,512,512]{2,1,0:T(8,128)(2,1)S(1)} custom-call(s32[4]{0:T(128)S(1)} %pad_add_fusion.1.part_ref, f32[3,2,512,512]{3,2,1,0:T(8,128)} %bitcast.14), custom_call_target="tpu_custom_call" | custom-call | flops 1048576 | bytes 1048576 | tf_op jit(solution)/shard_map/pallas_call | solution.py:276
  8.3 2.8 %collective-permute-start.22 = (bf16[1,512,512]{2,1,0:T(8,128)(2,1)S(1)}, bf16[1,512,512]{2,1,0:T(8,128)(2,1)S(1)}, u32[]{:S(2)}, u32[]{:S(2)}) collective-permute-start(bf16[1,512,512]{2,1,0:T(8,128)(2,1)S(1)} %get-tuple-element.52.refs_1_), channel_id=1, source_target_pairs={{0,1},{1,3},{2,0},{3,5},{4,2},{5,7},{6,4},{7,6},{8,9},{9,11},{10,8... | collective-permute-start | bytes 1572872 | tf_op jit(solution)/shard_map/ppermute | solution.py:236
  11.1 1.3 collective-permute-start.19
  12.7 2.2 %collective-permute-start.5 = (bf16[1,256,512]{2,1,0:T(8,128)(2,1)S(1)}, bf16[1,256,512]{2,1,0:T(8,128)(2,1)S(1)}, u32[]{:S(2)}, u32[]{:S(2)}) collective-permute-start(bf16[1,256,512]{2,1,0:T(8,128)(2,1)S(1)} %get-tuple-element.56), channel_id=1, source_target_pairs={{0,8},{1,17},{2,10},{3,19},{4,12},{5,21},{6,14},{7,23},{8,0},{9,25... | collective-permute-start | bytes 786440 | tf_op jit(solution)/shard_map/ppermute | solution.py:236
  15.0 4.3 %collective-permute-done.partner_ref = s32[3,12]{1,0:T(4,128)S(1)} collective-permute-done((s32[3,12]{1,0:T(4,128)S(1)}, s32[3,12]{1,0:T(4,128)S(1)}, u32[]{:S(2)}, u32[]{:S(2)}) %collective-permute-start) | collective-permute-done | bytes 176 | tf_op jit(solution)/shard_map/ppermute | solution.py:236
  19.3 2.0 %collective-permute-start.2 = (bf16[1,256,512]{2,1,0:T(8,128)(2,1)S(1)}, bf16[1,256,512]{2,1,0:T(8,128)(2,1)S(1)}, u32[]{:S(2)}, u32[]{:S(2)}) collective-permute-start(bf16[1,256,512]{2,1,0:T(8,128)(2,1)S(1)} %get-tuple-element.55), channel_id=1, source_target_pairs={{0,8},{1,17},{2,10},{3,19},{4,12},{5,21},{6,14},{7,23},{8,0},{9,25... | collective-permute-start | bytes 786440 | tf_op jit(solution)/shard_map/ppermute | solution.py:236
  21.3 1.6 %collective-permute-start.24 = (bf16[1,512,512]{2,1,0:T(8,128)(2,1)S(1)}, bf16[1,512,512]{2,1,0:T(8,128)(2,1)S(1)}, u32[]{:S(2)}, u32[]{:S(2)}) collective-permute-start(bf16[1,512,512]{2,1,0:T(8,128)(2,1)S(1)} %get-tuple-element.62.chosen), channel_id=1, source_target_pairs={{0,2},{1,0},{2,4},{3,1},{4,6},{5,3},{6,7},{7,5},{8,10},{9,8},{10,1... | collective-permute-start | bytes 1572872 | tf_op jit(solution)/shard_map/ppermute | solution.py:236
  22.9 1.0 collective-permute-done.22.gone
  23.8 2.4 %collective-permute-start.14 = (bf16[1,512,512]{2,1,0:T(8,128)(2,1)S(1)}, bf16[1,512,512]{2,1,0:T(8,128)(2,1)S(1)}, u32[]{:S(2)}, u32[]{:S(2)}) collective-permute-start(bf16[1,512,512]{2,1,0:T(8,128)(2,1)S(1)} %get-tuple-element.58), channel_id=1, source_target_pairs={{0,8},{1,17},{2,10},{3,19},{4,12},{5,21},{6,14},{7,23},{8,0},{9,25... | collective-permute-start | bytes 1572872 | tf_op jit(solution)/shard_map/ppermute | solution.py:236
  26.2 8.6 %collective-permute-done.19.gone = bf16[1,512,512]{2,1,0:T(8,128)(2,1)S(1)} collective-permute-done((bf16[1,512,512]{2,1,0:T(8,128)(2,1)S(1)}, bf16[1,512,512]{2,1,0:T(8,128)(2,1)S(1)}, u32[]{:S(2)}, u32[]{:S(2)}) %collective-permute-start.19) | collective-permute-done | bytes 524320 | tf_op jit(solution)/shard_map/ppermute | solution.py:236
  34.9 2.0 %collective-permute-start.21 = (bf16[1,512,512]{2,1,0:T(8,128)(2,1)S(1)}, bf16[1,512,512]{2,1,0:T(8,128)(2,1)S(1)}, u32[]{:S(2)}, u32[]{:S(2)}) collective-permute-start(bf16[1,512,512]{2,1,0:T(8,128)(2,1)S(1)} %get-tuple-element.61.chosen), channel_id=1, source_target_pairs={{0,2},{1,0},{2,4},{3,1},{4,6},{5,3},{6,7},{7,5},{8,10},{9,8},{10,1... | collective-permute-start | bytes 1572872 | tf_op jit(solution)/shard_map/ppermute | solution.py:236
  36.9 1.6 %collective-permute-start.18 = (bf16[1,512,512]{2,1,0:T(8,128)(2,1)S(1)}, bf16[1,512,512]{2,1,0:T(8,128)(2,1)S(1)}, u32[]{:S(2)}, u32[]{:S(2)}) collective-permute-start(bf16[1,512,512]{2,1,0:T(8,128)(2,1)S(1)} %get-tuple-element.60.chosen), channel_id=1, source_target_pairs={{0,2},{1,0},{2,4},{3,1},{4,6},{5,3},{6,7},{7,5},{8,10},{9,8},{10,1... | collective-permute-start | bytes 1572872 | tf_op jit(solution)/shard_map/ppermute | solution.py:236
  38.5 1.5 %collective-permute-start.10 = (bf16[1,512,512]{2,1,0:T(8,128)(2,1)S(1)}, bf16[1,512,512]{2,1,0:T(8,128)(2,1)S(1)}, u32[]{:S(2)}, u32[]{:S(2)}) collective-permute-start(bf16[1,512,512]{2,1,0:T(8,128)(2,1)S(1)} %get-tuple-element.57), channel_id=1, source_target_pairs={{0,8},{1,17},{2,10},{3,19},{4,12},{5,21},{6,14},{7,23},{8,0},{9,25... | collective-permute-start | bytes 1572872 | tf_op jit(solution)/shard_map/ppermute | solution.py:236
  40.0 0.8 collective-permute-start.15
  40.9 2.7 %collective-permute-done.21.came = bf16[1,512,512]{2,1,0:T(8,128)(2,1)S(1)} collective-permute-done((bf16[1,512,512]{2,1,0:T(8,128)(2,1)S(1)}, bf16[1,512,512]{2,1,0:T(8,128)(2,1)S(1)}, u32[]{:S(2)}, u32[]{:S(2)}) %collective-permute-start.21) | collective-permute-done | bytes 524320 | tf_op jit(solution)/shard_map/ppermute | solution.py:236
  43.6 11.1 %collective-permute-done.18.came = bf16[1,512,512]{2,1,0:T(8,128)(2,1)S(1)} collective-permute-done((bf16[1,512,512]{2,1,0:T(8,128)(2,1)S(1)}, bf16[1,512,512]{2,1,0:T(8,128)(2,1)S(1)}, u32[]{:S(2)}, u32[]{:S(2)}) %collective-permute-start.18) | collective-permute-done | bytes 524320 | tf_op jit(solution)/shard_map/ppermute | solution.py:236
  54.7 2.5 %collective-permute-start.3 = (bf16[1,256,512]{2,1,0:T(8,128)(2,1)S(1)}, bf16[1,256,512]{2,1,0:T(8,128)(2,1)S(1)}, u32[]{:S(2)}, u32[]{:S(2)}) collective-permute-start(bf16[1,256,512]{2,1,0:T(8,128)(2,1)S(1)} %collective-permute-done.2.chosen), channel_id=1, source_target_pairs={{0,2},{1,0},{2,4},{3,1},{4,6},{5,3},{6,7},{7,5},{8,10},{9,8},{10,1... | collective-permute-start | bytes 786440 | tf_op jit(solution)/shard_map/ppermute | solution.py:236
  57.2 3.1 %collective-permute-done.6.came = bf16[1,256,512]{2,1,0:T(8,128)(2,1)S(1)} collective-permute-done((bf16[1,256,512]{2,1,0:T(8,128)(2,1)S(1)}, bf16[1,256,512]{2,1,0:T(8,128)(2,1)S(1)}, u32[]{:S(2)}, u32[]{:S(2)}) %collective-permute-start.6) | collective-permute-done | bytes 262176 | tf_op jit(solution)/shard_map/ppermute | solution.py:236
  60.6 1.6 %collective-permute-start.26 = (bf16[1,512,512]{2,1,0:T(8,128)(2,1)S(1)}, bf16[1,512,512]{2,1,0:T(8,128)(2,1)S(1)}, u32[]{:S(2)}, u32[]{:S(2)}) collective-permute-start(bf16[1,512,512]{2,1,0:T(8,128)(2,1)S(1)} %shard_map.65.refs_0_), channel_id=1, source_target_pairs={{0,16},{1,9},{2,18},{3,11},{4,20},{5,13},{6,22},{7,15},{8,24},{9,1... | collective-permute-start | bytes 1572872 | tf_op jit(solution)/shard_map/ppermute | solution.py:236
  62.2 9.5 %collective-permute-done.3.came = bf16[1,256,512]{2,1,0:T(8,128)(2,1)S(1)} collective-permute-done((bf16[1,256,512]{2,1,0:T(8,128)(2,1)S(1)}, bf16[1,256,512]{2,1,0:T(8,128)(2,1)S(1)}, u32[]{:S(2)}, u32[]{:S(2)}) %collective-permute-start.3) | collective-permute-done | bytes 262176 | tf_op jit(solution)/shard_map/ppermute | solution.py:236
  71.7 4.4 %collective-permute-start.11 = (bf16[1,512,512]{2,1,0:T(8,128)(2,1)S(1)}, bf16[1,512,512]{2,1,0:T(8,128)(2,1)S(1)}, u32[]{:S(2)}, u32[]{:S(2)}) collective-permute-start(bf16[1,512,512]{2,1,0:T(8,128)(2,1)S(1)} %collective-permute-done.10.chosen), channel_id=1, source_target_pairs={{0,2},{1,0},{2,4},{3,1},{4,6},{5,3},{6,7},{7,5},{8,10},{9,8},{10,1... | collective-permute-start | bytes 1572872 | tf_op jit(solution)/shard_map/ppermute | solution.py:236
  76.4 1.6 %collective-permute-start.23 = (bf16[1,512,512]{2,1,0:T(8,128)(2,1)S(1)}, bf16[1,512,512]{2,1,0:T(8,128)(2,1)S(1)}, u32[]{:S(2)}, u32[]{:S(2)}) collective-permute-start(bf16[1,512,512]{2,1,0:T(8,128)(2,1)S(1)} %shard_map.64.refs_0_), channel_id=1, source_target_pairs={{0,16},{1,9},{2,18},{3,11},{4,20},{5,13},{6,22},{7,15},{8,24},{9,1... | collective-permute-start | bytes 1572872 | tf_op jit(solution)/shard_map/ppermute | solution.py:236
  77.9 0.3 shard_map.63.refs_0_
  78.3 0.6 collective-permute-start.20
  78.8 3.0 %shard_map.55 = (s32[5770]{0:T(1024)S(4)}, f32[7]{0:T(128)S(4)}) custom-call(s32[3,12]{1,0:T(4,128)S(1)} %broadcast_add_fusion.own_ref, s32[3,12]{1,0:T(4,128)S(1)} %collective-permute-done.partner_ref, f32[1]{0:T(128)S(6)} %copy.44.occupancy, s32[3]{0:T(128)S(1)} %add_convert_fusion.sides, s32[3]{0:T(128)S(1)} %pad_add_fusion.place_ref), custom_call_target="tpu_custom_call" | custom-call | flops 1048576 | bytes 1048576 | tf_op jit(solution)/shard_map/pallas_call | solution.py:276
  82.1 0.3 shard_map.62.refs_0_
  82.5 1.6 %collective-permute-start.17 = (bf16[1,512,512]{2,1,0:T(8,128)(2,1)S(1)}, bf16[1,512,512]{2,1,0:T(8,128)(2,1)S(1)}, u32[]{:S(2)}, u32[]{:S(2)}) collective-permute-start(bf16[1,512,512]{2,1,0:T(8,128)(2,1)S(1)} %shard_map.62.refs_0_), channel_id=1, source_target_pairs={{0,16},{1,9},{2,18},{3,11},{4,20},{5,13},{6,22},{7,15},{8,24},{9,1... | collective-permute-start | bytes 1572872 | tf_op jit(solution)/shard_map/ppermute | solution.py:236
  84.0 3.3 %shard_map.66 = (bf16[13,512,512]{2,1,0:T(8,128)(2,1)S(1)}, f32[6,512,512]{2,1,0:T(8,128)S(1)}) custom-call(s32[5770]{0:T(1024)S(4)} %get-tuple-element.47.table, bf16[9,512,512]{2,1,0:T(8,128)(2,1)S(1)} %bitcast.12, bf16[1,512,512]{2,1,0:T(8,128)(2,1)S(1)} %shard_map.65.refs_0_, bf16[1,512,512]{2,1,0:T(8,128)(2,1)S(1)} %collective-permute-done.26.refs_1_), custom_call_target="tpu_custom_call" | custom-call | flops 2684354560 | bytes 1048576 | tf_op jit(solution)/shard_map/pallas_call | solution.py:276
  87.5 2.0 %collective-permute-start.8 = (bf16[1,256,512]{2,1,0:T(8,128)(2,1)S(1)}, bf16[1,256,512]{2,1,0:T(8,128)(2,1)S(1)}, u32[]{:S(2)}, u32[]{:S(2)}) collective-permute-start(bf16[1,256,512]{2,1,0:T(8,128)(2,1)S(1)} %shard_map.59.refs_0_), channel_id=1, source_target_pairs={{0,16},{1,9},{2,18},{3,11},{4,20},{5,13},{6,22},{7,15},{8,24},{9,1... | collective-permute-start | bytes 786440 | tf_op jit(solution)/shard_map/ppermute | solution.py:236
  89.9 2.9 %shard_map.67 = (bf16[13,512,512]{2,1,0:T(8,128)(2,1)S(1)}, f32[6,512,512]{2,1,0:T(8,128)S(1)}) custom-call(s32[5770]{0:T(1024)S(4)} %get-tuple-element.47.table, bf16[9,512,512]{2,1,0:T(8,128)(2,1)S(1)} %bitcast.12, bf16[1,512,512]{2,1,0:T(8,128)(2,1)S(1)} %shard_map.64.refs_0_, ...), custom_call_target="tpu_custom_call", output_to_operand_aliasing={{0}: (4, {}), {1}: (5, {})} | custom-call | flops 2684354560 | bytes 1048576 | tf_op jit(solution)/shard_map/pallas_call | solution.py:276
  92.8 2.3 %shard_map.68 = (bf16[13,512,512]{2,1,0:T(8,128)(2,1)S(1)}, f32[6,512,512]{2,1,0:T(8,128)S(1)}) custom-call(s32[5770]{0:T(1024)S(4)} %get-tuple-element.47.table, bf16[9,512,512]{2,1,0:T(8,128)(2,1)S(1)} %bitcast.12, bf16[1,512,512]{2,1,0:T(8,128)(2,1)S(1)} %shard_map.63.refs_0_, ...), custom_call_target="tpu_custom_call", output_to_operand_aliasing={{0}: (4, {}), {1}: (5, {})} | custom-call | flops 2684354560 | bytes 1048576 | tf_op jit(solution)/shard_map/pallas_call | solution.py:276
  95.1 1.7 %collective-permute-done.17.refs_1_ = bf16[1,512,512]{2,1,0:T(8,128)(2,1)S(1)} collective-permute-done((bf16[1,512,512]{2,1,0:T(8,128)(2,1)S(1)}, bf16[1,512,512]{2,1,0:T(8,128)(2,1)S(1)}, u32[]{:S(2)}, u32[]{:S(2)}) %collective-permute-start.17) | collective-permute-done | bytes 524320 | tf_op jit(solution)/shard_map/ppermute | solution.py:236
  96.8 6.7 %shard_map.69 = (bf16[13,512,512]{2,1,0:T(8,128)(2,1)S(1)}, f32[6,512,512]{2,1,0:T(8,128)S(1)}) custom-call(s32[5770]{0:T(1024)S(4)} %get-tuple-element.47.table, bf16[9,512,512]{2,1,0:T(8,128)(2,1)S(1)} %bitcast.12, bf16[1,512,512]{2,1,0:T(8,128)(2,1)S(1)} %shard_map.62.refs_0_, ...), custom_call_target="tpu_custom_call", output_to_operand_aliasing={{0}: (4, {}), {1}: (5, {})} | custom-call | flops 2684354560 | bytes 1048576 | tf_op jit(solution)/shard_map/pallas_call | solution.py:276
  103.5 4.5 %collective-permute-done.13.refs_1_ = bf16[1,512,512]{2,1,0:T(8,128)(2,1)S(1)} collective-permute-done((bf16[1,512,512]{2,1,0:T(8,128)(2,1)S(1)}, bf16[1,512,512]{2,1,0:T(8,128)(2,1)S(1)}, u32[]{:S(2)}, u32[]{:S(2)}) %collective-permute-start.13) | collective-permute-done | bytes 524320 | tf_op jit(solution)/shard_map/ppermute | solution.py:236
  108.1 3.7 %shard_map.70 = (bf16[13,512,512]{2,1,0:T(8,128)(2,1)S(1)}, f32[6,512,512]{2,1,0:T(8,128)S(1)}) custom-call(s32[5770]{0:T(1024)S(4)} %get-tuple-element.47.table, bf16[9,512,512]{2,1,0:T(8,128)(2,1)S(1)} %bitcast.12, bf16[1,512,512]{2,1,0:T(8,128)(2,1)S(1)} %shard_map.61.refs_0_, ...), custom_call_target="tpu_custom_call", output_to_operand_aliasing={{0}: (4, {}), {1}: (5, {})} | custom-call | flops 2684354560 | bytes 1048576 | tf_op jit(solution)/shard_map/pallas_call | solution.py:276
  111.8 1.6 %shard_map.71 = (bf16[13,512,512]{2,1,0:T(8,128)(2,1)S(1)}, f32[6,512,512]{2,1,0:T(8,128)S(1)}, bf16[1,512,512]{2,1,0:T(8,128)(2,1)S(1)}) custom-call(s32[5770]{0:T(1024)S(4)} %get-tuple-element.47.table, bf16[9,512,512]{2,1,0:T(8,128)(2,1)S(1)} %bitcast.12, ...), custom_call_target="tpu_custom_call", output_to_operand_aliasing={{0}: (6, {}), {1}: (7, {})} | custom-call | flops 2684354560 | bytes 1048576 | tf_op jit(solution)/shard_map/pallas_call | solution.py:276
  113.4 1.5 %shard_map.72 = (bf16[13,512,512]{2,1,0:T(8,128)(2,1)S(1)}, f32[6,512,512]{2,1,0:T(8,128)S(1)}, bf16[1,512,512]{2,1,0:T(8,128)(2,1)S(1)}) custom-call(s32[5770]{0:T(1024)S(4)} %get-tuple-element.47.table, bf16[9,512,512]{2,1,0:T(8,128)(2,1)S(1)} %bitcast.12, ...), custom_call_target="tpu_custom_call", output_to_operand_aliasing={{0}: (2, {}), {1}: (3, {})} | custom-call | flops 1073741824 | bytes 1048576 | tf_op jit(solution)/shard_map/pallas_call | solution.py:276
  115.0 2.0 %collective-permute-start.28 = (bf16[1,512,512]{2,1,0:T(8,128)(2,1)S(1)}, bf16[1,512,512]{2,1,0:T(8,128)(2,1)S(1)}, u32[]{:S(2)}, u32[]{:S(2)}) collective-permute-start(bf16[1,512,512]{2,1,0:T(8,128)(2,1)S(1)} %get-tuple-element.78), channel_id=1, source_target_pairs={{0,8},{1,17},{2,10},{3,19},{4,12},{5,21},{6,14},{7,23},{8,0},{9,25... | collective-permute-start | bytes 1572872 | tf_op jit(solution)/shard_map/ppermute | solution.py:236
  117.0 1.5 %shard_map.73 = (bf16[13,512,512]{2,1,0:T(8,128)(2,1)S(1)}, f32[6,512,512]{2,1,0:T(8,128)S(1)}, bf16[1,512,512]{2,1,0:T(8,128)(2,1)S(1)}) custom-call(s32[5770]{0:T(1024)S(4)} %get-tuple-element.47.table, bf16[9,512,512]{2,1,0:T(8,128)(2,1)S(1)} %bitcast.12, ...), custom_call_target="tpu_custom_call", output_to_operand_aliasing={{0}: (2, {}), {1}: (3, {})} | custom-call | flops 1073741824 | bytes 1048576 | tf_op jit(solution)/shard_map/pallas_call | solution.py:276
  118.6 2.4 %shard_map.74 = (bf16[13,512,512]{2,1,0:T(8,128)(2,1)S(1)}, f32[6,512,512]{2,1,0:T(8,128)S(1)}) custom-call(s32[5770]{0:T(1024)S(4)} %get-tuple-element.47.table, bf16[9,512,512]{2,1,0:T(8,128)(2,1)S(1)} %bitcast.12, bf16[13,512,512]{2,1,0:T(8,128)(2,1)S(1)} %get-tuple-element.80.refs_0_, ...), custom_call_target="tpu_custom_call", output_to_operand_aliasing={{0}: (2, {}), {1}: (3, {})} | custom-call | flops 2684354560 | bytes 1048576 | tf_op jit(solution)/shard_map/pallas_call | solution.py:276
  121.1 5.8 %shard_map.75 = (f32[6,512,512]{2,1,0:T(8,128)S(1)}, f32[3,1,2,512,512]{4,3,2,1,0:T(8,128)}) custom-call(s32[5770]{0:T(1024)S(4)} %get-tuple-element.47.table, s32[1]{0:T(128)} %bitcast.7.part_ref, bf16[9,512,512]{2,1,0:T(8,128)(2,1)S(1)} %bitcast.12, bf16[13,512,512]{2,1,0:T(8,128)(2,1)S(1)} %get-tuple-element.82.blocks, ...), custom_call_target="tpu_custom_call", output_to_operand_aliasing={{0}: (4, {})} | custom-call | flops 1048576 | bytes 1048576 | tf_op jit(solution)/shard_map/pallas_call | solution.py:276
  126.9 2.9 %collective-permute-done.28.refs_0_ = bf16[1,512,512]{2,1,0:T(8,128)(2,1)S(1)} collective-permute-done((bf16[1,512,512]{2,1,0:T(8,128)(2,1)S(1)}, bf16[1,512,512]{2,1,0:T(8,128)(2,1)S(1)}, u32[]{:S(2)}, u32[]{:S(2)}) %collective-permute-start.28) | collective-permute-done | bytes 524320 | tf_op jit(solution)/shard_map/ppermute | solution.py:236
  129.7 1.4 %shard_map.76.refs_1_ = f32[3,1,2,512,512]{4,3,2,1,0:T(8,128)} custom-call(s32[1]{0:T(128)} %bitcast.part_ref, bf16[1,512,512]{2,1,0:T(8,128)(2,1)S(1)} %collective-permute-done.28.refs_0_, bf16[1,512,512]{2,1,0:T(8,128)(2,1)S(1)} %collective-permute-done.29.refs_1_, f32[3,1,2,512,512]{4,3,2,1,0:T(8,128)} %get-tuple-element.84.refs_2_), custom_call_target="tpu_custom_call", output_to_operand_aliasing={{}: (3, {})} | custom-call | flops 1048576 | bytes 1048576 | tf_op jit(solution)/shard_map/pallas_call | solution.py:276
  131.2 4.2 %collective-permute-done.27.refs_0_ = bf16[1,512,512]{2,1,0:T(8,128)(2,1)S(1)} collective-permute-done((bf16[1,512,512]{2,1,0:T(8,128)(2,1)S(1)}, bf16[1,512,512]{2,1,0:T(8,128)(2,1)S(1)}, u32[]{:S(2)}, u32[]{:S(2)}) %collective-permute-start.27) | collective-permute-done | bytes 524320 | tf_op jit(solution)/shard_map/ppermute | solution.py:236
  135.4 1.1 shard_map.77
  (51 shorter events, 2.4 us)
Async XLA Ops:
  0.9 0.7 copy-start
  1.5 10.8 %copy-start.1 = (s32[3]{0:T(128)S(1)}, s32[3]{0:T(128)}, u32[]{:S(2)}) copy-start(s32[3]{0:T(128)} %shift.1) | copy-start | bytes 40
  5.9 9.0 %copy-start.2 = (s32[3,12]{1,0:T(4,128)S(1)}, s32[3,12]{1,0:T(4,128)}, u32[]{:S(2)}) copy-start(s32[3,12]{1,0:T(4,128)} %param.6) | copy-start | bytes 436
  5.9 6.5 %collective-permute-start.1 = (bf16[6,512,512]{2,1,0:T(8,128)(2,1)S(1)}, bf16[6,512,512]{2,1,0:T(8,128)(2,1)S(1)}, u32[]{:S(2)}, u32[]{:S(2)}) collective-permute-start(bf16[6,512,512]{2,1,0:T(8,128)(2,1)S(1)} %get-tuple-element.51), channel_id=1, source_target_pairs={{0,1},{1,0},{2,3},{3,2},{4,5},{5,4},{6,7},{7,6},{8,9},{9,8},{10,11... | collective-permute-start | bytes 9437192 | tf_op jit(solution)/shard_map/ppermute | solution.py:236
  8.3 13.0 %collective-permute-start.25 = (bf16[1,512,512]{2,1,0:T(8,128)(2,1)S(1)}, bf16[1,512,512]{2,1,0:T(8,128)(2,1)S(1)}, u32[]{:S(2)}, u32[]{:S(2)}) collective-permute-start(bf16[1,512,512]{2,1,0:T(8,128)(2,1)S(1)} %shard_map.57.refs_0_), channel_id=1, source_target_pairs={{0,1},{1,3},{2,0},{3,5},{4,2},{5,7},{6,4},{7,6},{8,9},{9,11},{10,8... | collective-permute-start | bytes 1572872 | tf_op jit(solution)/shard_map/ppermute | solution.py:236
  8.3 15.6 %collective-permute-start.22 = (bf16[1,512,512]{2,1,0:T(8,128)(2,1)S(1)}, bf16[1,512,512]{2,1,0:T(8,128)(2,1)S(1)}, u32[]{:S(2)}, u32[]{:S(2)}) collective-permute-start(bf16[1,512,512]{2,1,0:T(8,128)(2,1)S(1)} %get-tuple-element.52.refs_1_), channel_id=1, source_target_pairs={{0,1},{1,3},{2,0},{3,5},{4,2},{5,7},{6,4},{7,6},{8,9},{9,11},{10,8... | collective-permute-start | bytes 1572872 | tf_op jit(solution)/shard_map/ppermute | solution.py:236
  11.1 23.8 %collective-permute-start.19 = (bf16[1,512,512]{2,1,0:T(8,128)(2,1)S(1)}, bf16[1,512,512]{2,1,0:T(8,128)(2,1)S(1)}, u32[]{:S(2)}, u32[]{:S(2)}) collective-permute-start(bf16[1,512,512]{2,1,0:T(8,128)(2,1)S(1)} %get-tuple-element.53.refs_2_), channel_id=1, source_target_pairs={{0,1},{1,3},{2,0},{3,5},{4,2},{5,7},{6,4},{7,6},{8,9},{9,11},{10,8... | collective-permute-start | bytes 1572872 | tf_op jit(solution)/shard_map/ppermute | solution.py:236
  12.4 71.7 %slice-start = ((s8[4718592]{0:T(1024)(128)(4,1)}), s8[4194304]{0:T(1024)(128)(4,1)S(1)}, s32[]{:S(2)}) async-start(s8[4718592]{0:T(1024)(128)(4,1)} %bitcast.11), calls=%async_computation | async-start | bytes 8388608
  12.7 24.2 %collective-permute-start.5 = (bf16[1,256,512]{2,1,0:T(8,128)(2,1)S(1)}, bf16[1,256,512]{2,1,0:T(8,128)(2,1)S(1)}, u32[]{:S(2)}, u32[]{:S(2)}) collective-permute-start(bf16[1,256,512]{2,1,0:T(8,128)(2,1)S(1)} %get-tuple-element.56), channel_id=1, source_target_pairs={{0,8},{1,17},{2,10},{3,19},{4,12},{5,21},{6,14},{7,23},{8,0},{9,25... | collective-permute-start | bytes 786440 | tf_op jit(solution)/shard_map/ppermute | solution.py:236
  15.0 4.3 %collective-permute-start = (s32[3,12]{1,0:T(4,128)S(1)}, s32[3,12]{1,0:T(4,128)S(1)}, u32[]{:S(2)}, u32[]{:S(2)}) collective-permute-start(s32[3,12]{1,0:T(4,128)S(1)} %broadcast_add_fusion.own_ref), channel_id=1, source_target_pairs={{0,8},{1,17},{2,10},{3,19},{4,12},{5,21},{6,14},{7,23},{8,0},{9,25... | collective-permute-start | bytes 440 | tf_op jit(solution)/shard_map/ppermute | solution.py:236
  19.3 19.2 %collective-permute-start.2 = (bf16[1,256,512]{2,1,0:T(8,128)(2,1)S(1)}, bf16[1,256,512]{2,1,0:T(8,128)(2,1)S(1)}, u32[]{:S(2)}, u32[]{:S(2)}) collective-permute-start(bf16[1,256,512]{2,1,0:T(8,128)(2,1)S(1)} %get-tuple-element.55), channel_id=1, source_target_pairs={{0,8},{1,17},{2,10},{3,19},{4,12},{5,21},{6,14},{7,23},{8,0},{9,25... | collective-permute-start | bytes 786440 | tf_op jit(solution)/shard_map/ppermute | solution.py:236
  21.3 18.7 %collective-permute-start.24 = (bf16[1,512,512]{2,1,0:T(8,128)(2,1)S(1)}, bf16[1,512,512]{2,1,0:T(8,128)(2,1)S(1)}, u32[]{:S(2)}, u32[]{:S(2)}) collective-permute-start(bf16[1,512,512]{2,1,0:T(8,128)(2,1)S(1)} %get-tuple-element.62.chosen), channel_id=1, source_target_pairs={{0,2},{1,0},{2,4},{3,1},{4,6},{5,3},{6,7},{7,5},{8,10},{9,8},{10,1... | collective-permute-start | bytes 1572872 | tf_op jit(solution)/shard_map/ppermute | solution.py:236
  23.8 16.2 %collective-permute-start.14 = (bf16[1,512,512]{2,1,0:T(8,128)(2,1)S(1)}, bf16[1,512,512]{2,1,0:T(8,128)(2,1)S(1)}, u32[]{:S(2)}, u32[]{:S(2)}) collective-permute-start(bf16[1,512,512]{2,1,0:T(8,128)(2,1)S(1)} %get-tuple-element.58), channel_id=1, source_target_pairs={{0,8},{1,17},{2,10},{3,19},{4,12},{5,21},{6,14},{7,23},{8,0},{9,25... | collective-permute-start | bytes 1572872 | tf_op jit(solution)/shard_map/ppermute | solution.py:236
  34.9 8.7 %collective-permute-start.21 = (bf16[1,512,512]{2,1,0:T(8,128)(2,1)S(1)}, bf16[1,512,512]{2,1,0:T(8,128)(2,1)S(1)}, u32[]{:S(2)}, u32[]{:S(2)}) collective-permute-start(bf16[1,512,512]{2,1,0:T(8,128)(2,1)S(1)} %get-tuple-element.61.chosen), channel_id=1, source_target_pairs={{0,2},{1,0},{2,4},{3,1},{4,6},{5,3},{6,7},{7,5},{8,10},{9,8},{10,1... | collective-permute-start | bytes 1572872 | tf_op jit(solution)/shard_map/ppermute | solution.py:236
  36.9 17.8 %collective-permute-start.18 = (bf16[1,512,512]{2,1,0:T(8,128)(2,1)S(1)}, bf16[1,512,512]{2,1,0:T(8,128)(2,1)S(1)}, u32[]{:S(2)}, u32[]{:S(2)}) collective-permute-start(bf16[1,512,512]{2,1,0:T(8,128)(2,1)S(1)} %get-tuple-element.60.chosen), channel_id=1, source_target_pairs={{0,2},{1,0},{2,4},{3,1},{4,6},{5,3},{6,7},{7,5},{8,10},{9,8},{10,1... | collective-permute-start | bytes 1572872 | tf_op jit(solution)/shard_map/ppermute | solution.py:236
  38.5 16.2 %collective-permute-start.10 = (bf16[1,512,512]{2,1,0:T(8,128)(2,1)S(1)}, bf16[1,512,512]{2,1,0:T(8,128)(2,1)S(1)}, u32[]{:S(2)}, u32[]{:S(2)}) collective-permute-start(bf16[1,512,512]{2,1,0:T(8,128)(2,1)S(1)} %get-tuple-element.57), channel_id=1, source_target_pairs={{0,8},{1,17},{2,10},{3,19},{4,12},{5,21},{6,14},{7,23},{8,0},{9,25... | collective-permute-start | bytes 1572872 | tf_op jit(solution)/shard_map/ppermute | solution.py:236
  40.0 20.4 %collective-permute-start.6 = (bf16[1,256,512]{2,1,0:T(8,128)(2,1)S(1)}, bf16[1,256,512]{2,1,0:T(8,128)(2,1)S(1)}, u32[]{:S(2)}, u32[]{:S(2)}) collective-permute-start(bf16[1,256,512]{2,1,0:T(8,128)(2,1)S(1)} %collective-permute-done.5.chosen), channel_id=1, source_target_pairs={{0,2},{1,0},{2,4},{3,1},{4,6},{5,3},{6,7},{7,5},{8,10},{9,8},{10,1... | collective-permute-start | bytes 786440 | tf_op jit(solution)/shard_map/ppermute | solution.py:236
  40.0 36.3 %collective-permute-start.15 = (bf16[1,512,512]{2,1,0:T(8,128)(2,1)S(1)}, bf16[1,512,512]{2,1,0:T(8,128)(2,1)S(1)}, u32[]{:S(2)}, u32[]{:S(2)}) collective-permute-start(bf16[1,512,512]{2,1,0:T(8,128)(2,1)S(1)} %collective-permute-done.14.chosen), channel_id=1, source_target_pairs={{0,2},{1,0},{2,4},{3,1},{4,6},{5,3},{6,7},{7,5},{8,10},{9,8},{10,1... | collective-permute-start | bytes 1572872 | tf_op jit(solution)/shard_map/ppermute | solution.py:236
  43.6 17.0 %collective-permute-start.7 = (bf16[1,256,512]{2,1,0:T(8,128)(2,1)S(1)}, bf16[1,256,512]{2,1,0:T(8,128)(2,1)S(1)}, u32[]{:S(2)}, u32[]{:S(2)}) collective-permute-start(bf16[1,256,512]{2,1,0:T(8,128)(2,1)S(1)} %collective-permute-done.5.chosen), channel_id=1, source_target_pairs={{0,1},{1,3},{2,0},{3,5},{4,2},{5,7},{6,4},{7,6},{8,9},{9,11},{10,8... | collective-permute-start | bytes 786440 | tf_op jit(solution)/shard_map/ppermute | solution.py:236
  54.7 23.6 %collective-permute-start.16 = (bf16[1,512,512]{2,1,0:T(8,128)(2,1)S(1)}, bf16[1,512,512]{2,1,0:T(8,128)(2,1)S(1)}, u32[]{:S(2)}, u32[]{:S(2)}) collective-permute-start(bf16[1,512,512]{2,1,0:T(8,128)(2,1)S(1)} %collective-permute-done.14.chosen), channel_id=1, source_target_pairs={{0,1},{1,3},{2,0},{3,5},{4,2},{5,7},{6,4},{7,6},{8,9},{9,11},{10,8... | collective-permute-start | bytes 1572872 | tf_op jit(solution)/shard_map/ppermute | solution.py:236
  54.7 17.0 %collective-permute-start.3 = (bf16[1,256,512]{2,1,0:T(8,128)(2,1)S(1)}, bf16[1,256,512]{2,1,0:T(8,128)(2,1)S(1)}, u32[]{:S(2)}, u32[]{:S(2)}) collective-permute-start(bf16[1,256,512]{2,1,0:T(8,128)(2,1)S(1)} %collective-permute-done.2.chosen), channel_id=1, source_target_pairs={{0,2},{1,0},{2,4},{3,1},{4,6},{5,3},{6,7},{7,5},{8,10},{9,8},{10,1... | collective-permute-start | bytes 786440 | tf_op jit(solution)/shard_map/ppermute | solution.py:236
  60.3 15.7 %collective-permute-start.4 = (bf16[1,256,512]{2,1,0:T(8,128)(2,1)S(1)}, bf16[1,256,512]{2,1,0:T(8,128)(2,1)S(1)}, u32[]{:S(2)}, u32[]{:S(2)}) collective-permute-start(bf16[1,256,512]{2,1,0:T(8,128)(2,1)S(1)} %collective-permute-done.2.chosen), channel_id=1, source_target_pairs={{0,1},{1,3},{2,0},{3,5},{4,2},{5,7},{6,4},{7,6},{8,9},{9,11},{10,8... | collective-permute-start | bytes 786440 | tf_op jit(solution)/shard_map/ppermute | solution.py:236
  60.3 23.7 %slice-start.1 = ((s8[4718592]{0:T(1024)(128)(4,1)}), s8[524288]{0:T(1024)(128)(4,1)S(1)}, s32[]{:S(2)}) async-start(s8[4718592]{0:T(1024)(128)(4,1)} %bitcast.11), calls=%async_computation.1 | async-start | bytes 1048576
  60.6 21.8 %collective-permute-start.26 = (bf16[1,512,512]{2,1,0:T(8,128)(2,1)S(1)}, bf16[1,512,512]{2,1,0:T(8,128)(2,1)S(1)}, u32[]{:S(2)}, u32[]{:S(2)}) collective-permute-start(bf16[1,512,512]{2,1,0:T(8,128)(2,1)S(1)} %shard_map.65.refs_0_), channel_id=1, source_target_pairs={{0,16},{1,9},{2,18},{3,11},{4,20},{5,13},{6,22},{7,15},{8,24},{9,1... | collective-permute-start | bytes 1572872 | tf_op jit(solution)/shard_map/ppermute | solution.py:236
  71.7 15.7 %collective-permute-start.11 = (bf16[1,512,512]{2,1,0:T(8,128)(2,1)S(1)}, bf16[1,512,512]{2,1,0:T(8,128)(2,1)S(1)}, u32[]{:S(2)}, u32[]{:S(2)}) collective-permute-start(bf16[1,512,512]{2,1,0:T(8,128)(2,1)S(1)} %collective-permute-done.10.chosen), channel_id=1, source_target_pairs={{0,2},{1,0},{2,4},{3,1},{4,6},{5,3},{6,7},{7,5},{8,10},{9,8},{10,1... | collective-permute-start | bytes 1572872 | tf_op jit(solution)/shard_map/ppermute | solution.py:236
  76.0 11.4 %collective-permute-start.12 = (bf16[1,512,512]{2,1,0:T(8,128)(2,1)S(1)}, bf16[1,512,512]{2,1,0:T(8,128)(2,1)S(1)}, u32[]{:S(2)}, u32[]{:S(2)}) collective-permute-start(bf16[1,512,512]{2,1,0:T(8,128)(2,1)S(1)} %collective-permute-done.10.chosen), channel_id=1, source_target_pairs={{0,1},{1,3},{2,0},{3,5},{4,2},{5,7},{6,4},{7,6},{8,9},{9,11},{10,8... | collective-permute-start | bytes 1572872 | tf_op jit(solution)/shard_map/ppermute | solution.py:236
  76.4 13.4 %collective-permute-start.23 = (bf16[1,512,512]{2,1,0:T(8,128)(2,1)S(1)}, bf16[1,512,512]{2,1,0:T(8,128)(2,1)S(1)}, u32[]{:S(2)}, u32[]{:S(2)}) collective-permute-start(bf16[1,512,512]{2,1,0:T(8,128)(2,1)S(1)} %shard_map.64.refs_0_), channel_id=1, source_target_pairs={{0,16},{1,9},{2,18},{3,11},{4,20},{5,13},{6,22},{7,15},{8,24},{9,1... | collective-permute-start | bytes 1572872 | tf_op jit(solution)/shard_map/ppermute | solution.py:236
  78.3 14.6 %collective-permute-start.20 = (bf16[1,512,512]{2,1,0:T(8,128)(2,1)S(1)}, bf16[1,512,512]{2,1,0:T(8,128)(2,1)S(1)}, u32[]{:S(2)}, u32[]{:S(2)}) collective-permute-start(bf16[1,512,512]{2,1,0:T(8,128)(2,1)S(1)} %shard_map.63.refs_0_), channel_id=1, source_target_pairs={{0,16},{1,9},{2,18},{3,11},{4,20},{5,13},{6,22},{7,15},{8,24},{9,1... | collective-permute-start | bytes 1572872 | tf_op jit(solution)/shard_map/ppermute | solution.py:236
  82.5 14.4 %collective-permute-start.17 = (bf16[1,512,512]{2,1,0:T(8,128)(2,1)S(1)}, bf16[1,512,512]{2,1,0:T(8,128)(2,1)S(1)}, u32[]{:S(2)}, u32[]{:S(2)}) collective-permute-start(bf16[1,512,512]{2,1,0:T(8,128)(2,1)S(1)} %shard_map.62.refs_0_), channel_id=1, source_target_pairs={{0,16},{1,9},{2,18},{3,11},{4,20},{5,13},{6,22},{7,15},{8,24},{9,1... | collective-permute-start | bytes 1572872 | tf_op jit(solution)/shard_map/ppermute | solution.py:236
  87.4 24.4 %collective-permute-start.9 = (bf16[1,256,512]{2,1,0:T(8,128)(2,1)S(1)}, bf16[1,256,512]{2,1,0:T(8,128)(2,1)S(1)}, u32[]{:S(2)}, u32[]{:S(2)}) collective-permute-start(bf16[1,256,512]{2,1,0:T(8,128)(2,1)S(1)} %shard_map.60.refs_1_), channel_id=1, source_target_pairs={{0,16},{1,9},{2,18},{3,11},{4,20},{5,13},{6,22},{7,15},{8,24},{9,1... | collective-permute-start | bytes 786440 | tf_op jit(solution)/shard_map/ppermute | solution.py:236
  87.5 24.3 %collective-permute-start.8 = (bf16[1,256,512]{2,1,0:T(8,128)(2,1)S(1)}, bf16[1,256,512]{2,1,0:T(8,128)(2,1)S(1)}, u32[]{:S(2)}, u32[]{:S(2)}) collective-permute-start(bf16[1,256,512]{2,1,0:T(8,128)(2,1)S(1)} %shard_map.59.refs_0_), channel_id=1, source_target_pairs={{0,16},{1,9},{2,18},{3,11},{4,20},{5,13},{6,22},{7,15},{8,24},{9,1... | collective-permute-start | bytes 786440 | tf_op jit(solution)/shard_map/ppermute | solution.py:236
  89.8 18.3 %collective-permute-start.13 = (bf16[1,512,512]{2,1,0:T(8,128)(2,1)S(1)}, bf16[1,512,512]{2,1,0:T(8,128)(2,1)S(1)}, u32[]{:S(2)}, u32[]{:S(2)}) collective-permute-start(bf16[1,512,512]{2,1,0:T(8,128)(2,1)S(1)} %shard_map.61.refs_0_), channel_id=1, source_target_pairs={{0,16},{1,9},{2,18},{3,11},{4,20},{5,13},{6,22},{7,15},{8,24},{9,1... | collective-permute-start | bytes 1572872 | tf_op jit(solution)/shard_map/ppermute | solution.py:236
  114.9 12.0 %collective-permute-start.29 = (bf16[1,512,512]{2,1,0:T(8,128)(2,1)S(1)}, bf16[1,512,512]{2,1,0:T(8,128)(2,1)S(1)}, u32[]{:S(2)}, u32[]{:S(2)}) collective-permute-start(bf16[1,512,512]{2,1,0:T(8,128)(2,1)S(1)} %get-tuple-element.79), channel_id=1, source_target_pairs={{0,8},{1,17},{2,10},{3,19},{4,12},{5,21},{6,14},{7,23},{8,0},{9,25... | collective-permute-start | bytes 1572872 | tf_op jit(solution)/shard_map/ppermute | solution.py:236
  115.0 14.8 %collective-permute-start.28 = (bf16[1,512,512]{2,1,0:T(8,128)(2,1)S(1)}, bf16[1,512,512]{2,1,0:T(8,128)(2,1)S(1)}, u32[]{:S(2)}, u32[]{:S(2)}) collective-permute-start(bf16[1,512,512]{2,1,0:T(8,128)(2,1)S(1)} %get-tuple-element.78), channel_id=1, source_target_pairs={{0,8},{1,17},{2,10},{3,19},{4,12},{5,21},{6,14},{7,23},{8,0},{9,25... | collective-permute-start | bytes 1572872 | tf_op jit(solution)/shard_map/ppermute | solution.py:236
  118.5 16.9 %collective-permute-start.27 = (bf16[1,512,512]{2,1,0:T(8,128)(2,1)S(1)}, bf16[1,512,512]{2,1,0:T(8,128)(2,1)S(1)}, u32[]{:S(2)}, u32[]{:S(2)}) collective-permute-start(bf16[1,512,512]{2,1,0:T(8,128)(2,1)S(1)} %get-tuple-element.77), channel_id=1, source_target_pairs={{0,8},{1,17},{2,10},{3,19},{4,12},{5,21},{6,14},{7,23},{8,0},{9,25... | collective-permute-start | bytes 1572872 | tf_op jit(solution)/shard_map/ppermute | solution.py:236

commit v2 on v1

--- a/solution.py
+++ b/solution.py
@@ -75,9 +75,9 @@
                 upto = jnp.minimum(MEMBERS, have - j * MEMBERS)
                 stage = lax.div(member[first + upto - 1], ways)
                 last = 2 * local - 1
-                call = jnp.where(stage == last, last + 1 + min(k, local), stage)
+                call = jnp.where(stage == last, last + 2 + min(k, local), stage)
                 if k >= local:
-                    call = jnp.where(stage == last - 1, last, call)
+                    call = call + jnp.where((stage == last - 1) | (stage == last - 2), 2, 0)
                 place = filled[call]
                 filled[call] = place + 1
                 table[call] = place + 1
@@ -257,7 +257,7 @@
         ways = 1 << bits
         slots = 2 * local * ways
         last = 2 * local - 1
-        calls = last + local + 2
+        calls = last + local + 3
         low = jnp.bfloat16
         scale = 1.0 / momenta
         m, e = lax.axis_index("mom"), lax.axis_index("en")
@@ -426,13 +426,15 @@
                     arrived.append(sends(values, gather_bit(bit)))
             arrived = [piece for values in arrived for piece in values]
             sends_now = [0] if call == last else []
-            state, sent = stage(call + (call == last), arrived, state, sends_now, 5, call * ways)
+            if call == last - 1:
+                state, _ = stage(last, [], state, [], 3)
+            state, sent = stage(call + 2 * (call == last), arrived, state, sends_now, 5, call * ways)
         got = []
         for k in range(local):
             if k:
-                state, sent = stage(last + 1 + k, [], state, [k], 2)
+                state, sent = stage(last + 2 + k, [], state, [k], 2)
             got.append(send(sent[0], partner))
-        state, _ = stage(last, [], state, [], 5)
+        state, _ = stage(last + 1, [], state, [], 5)
 
         hbm = pl.BlockSpec(memory_space=pltpu.HBM)
         out_shape = jax.ShapeDtypeStruct(green_blocks.shape, jnp.float32)
@@ -441,7 +443,7 @@
             pltpu.SemaphoreType.DMA((local,)),
         ]
         _, result = kernel(
-            functools.partial(finish_kernel, last + 1 + local, calls, scale),
+            functools.partial(finish_kernel, last + 2 + local, calls, scale),
             table,
             mine.reshape(1),
             weights,

time: 138 us -> 138 us (level)
    pallas_call x23 -> x24, Pallas kernels: 45.3 us -> 45.4 us  [kernel(): pl.pallas_call(act, compiler_params=pltpu.CompilerParams(vmem_limit_bytes...]
where the time goes in v2:
time: 138 us; the launch traced here: 137 us
  waiting for transfers between devices  53.6 us (39%)
  Pallas kernels  45.4 us (33%)
  starting transfers between devices  35.5 us (26%)
    ppermute x30, waiting for transfers between devices, move(): return lax.ppermute(value, both, pairs)  53.6 us
    pallas_call x24, Pallas kernels, kernel(): pl.pallas_call(act, compiler_params=pltpu.CompilerParams(vmem_limit_bytes...  45.4 us
    ppermute x30, starting transfers between devices, move(): return lax.ppermute(value, both, pairs)  35.5 us
  transfers between devices with their start and end apart: 30, of which 11 were waited for; matrix products, arithmetic and copies ran while one was open for 0% of the time, Pallas kernels for 27%

profile of v2, /device:TPU:0, one launch (start us, length us, event | category | flops | bytes accessed | tf_op | source)
XLA Modules:
  0.0 136.6 jit_solution(12542445555535505811)
XLA Ops:
  0.9 0.6 copy-done
  1.5 4.3 %shard_map.56 = (bf16[1,512,512]{2,1,0:T(8,128)(2,1)S(1)}, bf16[1,512,512]{2,1,0:T(8,128)(2,1)S(1)}, bf16[3,512,512]{2,1,0:T(8,128)(2,1)S(1)}, bf16[6,512,512]{2...) custom-call(s32[4]{0:T(128)S(1)} %pad_add_fusion.1.part_ref, s32[3]{0:T(128)S(1)} %copy-done, f32[1]{0:T(128)S(6)} %copy.48.occupancy, ...), custom_call_target="tpu_custom_call" | custom-call | flops 1048576 | bytes 1048576 | tf_op jit(solution)/shard_map/pallas_call | solution.py:276
  5.9 0.6 collective-permute-start.1
  6.4 1.8 %shard_map.57.refs_0_ = bf16[1,512,512]{2,1,0:T(8,128)(2,1)S(1)} custom-call(s32[4]{0:T(128)S(1)} %pad_add_fusion.1.part_ref, f32[3,2,512,512]{3,2,1,0:T(8,128)} %bitcast.14), custom_call_target="tpu_custom_call" | custom-call | flops 1048576 | bytes 1048576 | tf_op jit(solution)/shard_map/pallas_call | solution.py:276
  8.3 2.8 %collective-permute-start.22 = (bf16[1,512,512]{2,1,0:T(8,128)(2,1)S(1)}, bf16[1,512,512]{2,1,0:T(8,128)(2,1)S(1)}, u32[]{:S(2)}, u32[]{:S(2)}) collective-permute-start(bf16[1,512,512]{2,1,0:T(8,128)(2,1)S(1)} %get-tuple-element.54.refs_1_), channel_id=1, source_target_pairs={{0,1},{1,3},{2,0},{3,5},{4,2},{5,7},{6,4},{7,6},{8,9},{9,11},{10,8... | collective-permute-start | bytes 1572872 | tf_op jit(solution)/shard_map/ppermute | solution.py:236
  11.1 1.3 collective-permute-start.19
  12.7 2.2 %collective-permute-start.5 = (bf16[1,256,512]{2,1,0:T(8,128)(2,1)S(1)}, bf16[1,256,512]{2,1,0:T(8,128)(2,1)S(1)}, u32[]{:S(2)}, u32[]{:S(2)}) collective-permute-start(bf16[1,256,512]{2,1,0:T(8,128)(2,1)S(1)} %get-tuple-element.58), channel_id=1, source_target_pairs={{0,8},{1,17},{2,10},{3,19},{4,12},{5,21},{6,14},{7,23},{8,0},{9,25... | collective-permute-start | bytes 786440 | tf_op jit(solution)/shard_map/ppermute | solution.py:236
  15.0 4.3 %collective-permute-done.partner_ref = s32[3,12]{1,0:T(4,128)S(1)} collective-permute-done((s32[3,12]{1,0:T(4,128)S(1)}, s32[3,12]{1,0:T(4,128)S(1)}, u32[]{:S(2)}, u32[]{:S(2)}) %collective-permute-start) | collective-permute-done | bytes 176 | tf_op jit(solution)/shard_map/ppermute | solution.py:236
  19.3 2.0 %collective-permute-start.2 = (bf16[1,256,512]{2,1,0:T(8,128)(2,1)S(1)}, bf16[1,256,512]{2,1,0:T(8,128)(2,1)S(1)}, u32[]{:S(2)}, u32[]{:S(2)}) collective-permute-start(bf16[1,256,512]{2,1,0:T(8,128)(2,1)S(1)} %get-tuple-element.57), channel_id=1, source_target_pairs={{0,8},{1,17},{2,10},{3,19},{4,12},{5,21},{6,14},{7,23},{8,0},{9,25... | collective-permute-start | bytes 786440 | tf_op jit(solution)/shard_map/ppermute | solution.py:236
  21.3 1.6 %collective-permute-start.24 = (bf16[1,512,512]{2,1,0:T(8,128)(2,1)S(1)}, bf16[1,512,512]{2,1,0:T(8,128)(2,1)S(1)}, u32[]{:S(2)}, u32[]{:S(2)}) collective-permute-start(bf16[1,512,512]{2,1,0:T(8,128)(2,1)S(1)} %get-tuple-element.64.chosen), channel_id=1, source_target_pairs={{0,2},{1,0},{2,4},{3,1},{4,6},{5,3},{6,7},{7,5},{8,10},{9,8},{10,1... | collective-permute-start | bytes 1572872 | tf_op jit(solution)/shard_map/ppermute | solution.py:236
  22.9 1.0 collective-permute-done.22.gone
  23.8 2.4 %collective-permute-start.14 = (bf16[1,512,512]{2,1,0:T(8,128)(2,1)S(1)}, bf16[1,512,512]{2,1,0:T(8,128)(2,1)S(1)}, u32[]{:S(2)}, u32[]{:S(2)}) collective-permute-start(bf16[1,512,512]{2,1,0:T(8,128)(2,1)S(1)} %get-tuple-element.60), channel_id=1, source_target_pairs={{0,8},{1,17},{2,10},{3,19},{4,12},{5,21},{6,14},{7,23},{8,0},{9,25... | collective-permute-start | bytes 1572872 | tf_op jit(solution)/shard_map/ppermute | solution.py:236
  26.2 8.6 %collective-permute-done.19.gone = bf16[1,512,512]{2,1,0:T(8,128)(2,1)S(1)} collective-permute-done((bf16[1,512,512]{2,1,0:T(8,128)(2,1)S(1)}, bf16[1,512,512]{2,1,0:T(8,128)(2,1)S(1)}, u32[]{:S(2)}, u32[]{:S(2)}) %collective-permute-start.19) | collective-permute-done | bytes 524320 | tf_op jit(solution)/shard_map/ppermute | solution.py:236
  34.9 2.0 %collective-permute-start.21 = (bf16[1,512,512]{2,1,0:T(8,128)(2,1)S(1)}, bf16[1,512,512]{2,1,0:T(8,128)(2,1)S(1)}, u32[]{:S(2)}, u32[]{:S(2)}) collective-permute-start(bf16[1,512,512]{2,1,0:T(8,128)(2,1)S(1)} %get-tuple-element.63.chosen), channel_id=1, source_target_pairs={{0,2},{1,0},{2,4},{3,1},{4,6},{5,3},{6,7},{7,5},{8,10},{9,8},{10,1... | collective-permute-start | bytes 1572872 | tf_op jit(solution)/shard_map/ppermute | solution.py:236
  36.9 1.6 %collective-permute-start.18 = (bf16[1,512,512]{2,1,0:T(8,128)(2,1)S(1)}, bf16[1,512,512]{2,1,0:T(8,128)(2,1)S(1)}, u32[]{:S(2)}, u32[]{:S(2)}) collective-permute-start(bf16[1,512,512]{2,1,0:T(8,128)(2,1)S(1)} %get-tuple-element.62.chosen), channel_id=1, source_target_pairs={{0,2},{1,0},{2,4},{3,1},{4,6},{5,3},{6,7},{7,5},{8,10},{9,8},{10,1... | collective-permute-start | bytes 1572872 | tf_op jit(solution)/shard_map/ppermute | solution.py:236
  38.5 1.5 %collective-permute-start.10 = (bf16[1,512,512]{2,1,0:T(8,128)(2,1)S(1)}, bf16[1,512,512]{2,1,0:T(8,128)(2,1)S(1)}, u32[]{:S(2)}, u32[]{:S(2)}) collective-permute-start(bf16[1,512,512]{2,1,0:T(8,128)(2,1)S(1)} %get-tuple-element.59), channel_id=1, source_target_pairs={{0,8},{1,17},{2,10},{3,19},{4,12},{5,21},{6,14},{7,23},{8,0},{9,25... | collective-permute-start | bytes 1572872 | tf_op jit(solution)/shard_map/ppermute | solution.py:236
  40.0 0.8 collective-permute-start.15
  40.9 2.7 %collective-permute-done.21.came = bf16[1,512,512]{2,1,0:T(8,128)(2,1)S(1)} collective-permute-done((bf16[1,512,512]{2,1,0:T(8,128)(2,1)S(1)}, bf16[1,512,512]{2,1,0:T(8,128)(2,1)S(1)}, u32[]{:S(2)}, u32[]{:S(2)}) %collective-permute-start.21) | collective-permute-done | bytes 524320 | tf_op jit(solution)/shard_map/ppermute | solution.py:236
  43.6 11.1 %collective-permute-done.18.came = bf16[1,512,512]{2,1,0:T(8,128)(2,1)S(1)} collective-permute-done((bf16[1,512,512]{2,1,0:T(8,128)(2,1)S(1)}, bf16[1,512,512]{2,1,0:T(8,128)(2,1)S(1)}, u32[]{:S(2)}, u32[]{:S(2)}) %collective-permute-start.18) | collective-permute-done | bytes 524320 | tf_op jit(solution)/shard_map/ppermute | solution.py:236
  54.7 2.5 %collective-permute-start.3 = (bf16[1,256,512]{2,1,0:T(8,128)(2,1)S(1)}, bf16[1,256,512]{2,1,0:T(8,128)(2,1)S(1)}, u32[]{:S(2)}, u32[]{:S(2)}) collective-permute-start(bf16[1,256,512]{2,1,0:T(8,128)(2,1)S(1)} %collective-permute-done.2.chosen), channel_id=1, source_target_pairs={{0,2},{1,0},{2,4},{3,1},{4,6},{5,3},{6,7},{7,5},{8,10},{9,8},{10,1... | collective-permute-start | bytes 786440 | tf_op jit(solution)/shard_map/ppermute | solution.py:236
  57.2 3.1 %collective-permute-done.6.came = bf16[1,256,512]{2,1,0:T(8,128)(2,1)S(1)} collective-permute-done((bf16[1,256,512]{2,1,0:T(8,128)(2,1)S(1)}, bf16[1,256,512]{2,1,0:T(8,128)(2,1)S(1)}, u32[]{:S(2)}, u32[]{:S(2)}) %collective-permute-start.6) | collective-permute-done | bytes 262176 | tf_op jit(solution)/shard_map/ppermute | solution.py:236
  60.6 1.6 %collective-permute-start.26 = (bf16[1,512,512]{2,1,0:T(8,128)(2,1)S(1)}, bf16[1,512,512]{2,1,0:T(8,128)(2,1)S(1)}, u32[]{:S(2)}, u32[]{:S(2)}) collective-permute-start(bf16[1,512,512]{2,1,0:T(8,128)(2,1)S(1)} %shard_map.65.refs_0_), channel_id=1, source_target_pairs={{0,16},{1,9},{2,18},{3,11},{4,20},{5,13},{6,22},{7,15},{8,24},{9,1... | collective-permute-start | bytes 1572872 | tf_op jit(solution)/shard_map/ppermute | solution.py:236
  62.2 9.5 %collective-permute-done.3.came = bf16[1,256,512]{2,1,0:T(8,128)(2,1)S(1)} collective-permute-done((bf16[1,256,512]{2,1,0:T(8,128)(2,1)S(1)}, bf16[1,256,512]{2,1,0:T(8,128)(2,1)S(1)}, u32[]{:S(2)}, u32[]{:S(2)}) %collective-permute-start.3) | collective-permute-done | bytes 262176 | tf_op jit(solution)/shard_map/ppermute | solution.py:236
  71.7 4.4 %collective-permute-start.11 = (bf16[1,512,512]{2,1,0:T(8,128)(2,1)S(1)}, bf16[1,512,512]{2,1,0:T(8,128)(2,1)S(1)}, u32[]{:S(2)}, u32[]{:S(2)}) collective-permute-start(bf16[1,512,512]{2,1,0:T(8,128)(2,1)S(1)} %collective-permute-done.10.chosen), channel_id=1, source_target_pairs={{0,2},{1,0},{2,4},{3,1},{4,6},{5,3},{6,7},{7,5},{8,10},{9,8},{10,1... | collective-permute-start | bytes 1572872 | tf_op jit(solution)/shard_map/ppermute | solution.py:236
  76.4 1.6 %collective-permute-start.23 = (bf16[1,512,512]{2,1,0:T(8,128)(2,1)S(1)}, bf16[1,512,512]{2,1,0:T(8,128)(2,1)S(1)}, u32[]{:S(2)}, u32[]{:S(2)}) collective-permute-start(bf16[1,512,512]{2,1,0:T(8,128)(2,1)S(1)} %shard_map.64.refs_0_), channel_id=1, source_target_pairs={{0,16},{1,9},{2,18},{3,11},{4,20},{5,13},{6,22},{7,15},{8,24},{9,1... | collective-permute-start | bytes 1572872 | tf_op jit(solution)/shard_map/ppermute | solution.py:236
  77.9 0.3 shard_map.63.refs_0_
  78.3 0.6 collective-permute-start.20
  78.8 3.0 %shard_map.55 = (s32[6347]{0:T(1024)S(4)}, f32[7]{0:T(128)S(4)}) custom-call(s32[3,12]{1,0:T(4,128)S(1)} %broadcast_add_fusion.own_ref, s32[3,12]{1,0:T(4,128)S(1)} %collective-permute-done.partner_ref, f32[1]{0:T(128)S(6)} %copy.48.occupancy, s32[3]{0:T(128)S(1)} %add_convert_fusion.sides, s32[3]{0:T(128)S(1)} %pad_add_fusion.place_ref), custom_call_target="tpu_custom_call" | custom-call | flops 1048576 | bytes 1048576 | tf_op jit(solution)/shard_map/pallas_call | solution.py:276
  82.5 1.6 %collective-permute-start.17 = (bf16[1,512,512]{2,1,0:T(8,128)(2,1)S(1)}, bf16[1,512,512]{2,1,0:T(8,128)(2,1)S(1)}, u32[]{:S(2)}, u32[]{:S(2)}) collective-permute-start(bf16[1,512,512]{2,1,0:T(8,128)(2,1)S(1)} %shard_map.62.refs_0_), channel_id=1, source_target_pairs={{0,16},{1,9},{2,18},{3,11},{4,20},{5,13},{6,22},{7,15},{8,24},{9,1... | collective-permute-start | bytes 1572872 | tf_op jit(solution)/shard_map/ppermute | solution.py:236
  84.1 3.3 %shard_map.66 = (bf16[13,512,512]{2,1,0:T(8,128)(2,1)S(1)}, f32[6,512,512]{2,1,0:T(8,128)S(1)}) custom-call(s32[6347]{0:T(1024)S(4)} %get-tuple-element.49.table, bf16[9,512,512]{2,1,0:T(8,128)(2,1)S(1)} %bitcast.12, bf16[1,512,512]{2,1,0:T(8,128)(2,1)S(1)} %shard_map.65.refs_0_, bf16[1,512,512]{2,1,0:T(8,128)(2,1)S(1)} %collective-permute-done.26.refs_1_), custom_call_target="tpu_custom_call" | custom-call | flops 2684354560 | bytes 1048576 | tf_op jit(solution)/shard_map/pallas_call | solution.py:276
  87.5 2.0 %collective-permute-start.8 = (bf16[1,256,512]{2,1,0:T(8,128)(2,1)S(1)}, bf16[1,256,512]{2,1,0:T(8,128)(2,1)S(1)}, u32[]{:S(2)}, u32[]{:S(2)}) collective-permute-start(bf16[1,256,512]{2,1,0:T(8,128)(2,1)S(1)} %shard_map.59.refs_0_), channel_id=1, source_target_pairs={{0,16},{1,9},{2,18},{3,11},{4,20},{5,13},{6,22},{7,15},{8,24},{9,1... | collective-permute-start | bytes 786440 | tf_op jit(solution)/shard_map/ppermute | solution.py:236
  90.0 2.9 %shard_map.67 = (bf16[13,512,512]{2,1,0:T(8,128)(2,1)S(1)}, f32[6,512,512]{2,1,0:T(8,128)S(1)}) custom-call(s32[6347]{0:T(1024)S(4)} %get-tuple-element.49.table, bf16[9,512,512]{2,1,0:T(8,128)(2,1)S(1)} %bitcast.12, bf16[1,512,512]{2,1,0:T(8,128)(2,1)S(1)} %shard_map.64.refs_0_, ...), custom_call_target="tpu_custom_call", output_to_operand_aliasing={{0}: (4, {}), {1}: (5, {})} | custom-call | flops 2684354560 | bytes 1048576 | tf_op jit(solution)/shard_map/pallas_call | solution.py:276
  92.9 2.3 %shard_map.68 = (bf16[13,512,512]{2,1,0:T(8,128)(2,1)S(1)}, f32[6,512,512]{2,1,0:T(8,128)S(1)}) custom-call(s32[6347]{0:T(1024)S(4)} %get-tuple-element.49.table, bf16[9,512,512]{2,1,0:T(8,128)(2,1)S(1)} %bitcast.12, bf16[1,512,512]{2,1,0:T(8,128)(2,1)S(1)} %shard_map.63.refs_0_, ...), custom_call_target="tpu_custom_call", output_to_operand_aliasing={{0}: (4, {}), {1}: (5, {})} | custom-call | flops 2684354560 | bytes 1048576 | tf_op jit(solution)/shard_map/pallas_call | solution.py:276
  95.2 1.7 %collective-permute-done.17.refs_1_ = bf16[1,512,512]{2,1,0:T(8,128)(2,1)S(1)} collective-permute-done((bf16[1,512,512]{2,1,0:T(8,128)(2,1)S(1)}, bf16[1,512,512]{2,1,0:T(8,128)(2,1)S(1)}, u32[]{:S(2)}, u32[]{:S(2)}) %collective-permute-start.17) | collective-permute-done | bytes 524320 | tf_op jit(solution)/shard_map/ppermute | solution.py:236
  96.8 3.1 %shard_map.69 = (bf16[13,512,512]{2,1,0:T(8,128)(2,1)S(1)}, f32[6,512,512]{2,1,0:T(8,128)S(1)}) custom-call(s32[6347]{0:T(1024)S(4)} %get-tuple-element.49.table, bf16[9,512,512]{2,1,0:T(8,128)(2,1)S(1)} %bitcast.12, bf16[1,512,512]{2,1,0:T(8,128)(2,1)S(1)} %shard_map.62.refs_0_, ...), custom_call_target="tpu_custom_call", output_to_operand_aliasing={{0}: (4, {}), {1}: (5, {})} | custom-call | flops 2684354560 | bytes 1048576 | tf_op jit(solution)/shard_map/pallas_call | solution.py:276
  99.9 3.6 %shard_map.70 = (bf16[13,512,512]{2,1,0:T(8,128)(2,1)S(1)}, f32[6,512,512]{2,1,0:T(8,128)S(1)}) custom-call(s32[6347]{0:T(1024)S(4)} %get-tuple-element.49.table, bf16[9,512,512]{2,1,0:T(8,128)(2,1)S(1)} %bitcast.12, bf16[13,512,512]{2,1,0:T(8,128)(2,1)S(1)} %get-tuple-element.71.refs_0_, ...), custom_call_target="tpu_custom_call", output_to_operand_aliasing={{0}: (2, {}), {1}: (3, {})} | custom-call | flops 1610612736 | bytes 1048576 | tf_op jit(solution)/shard_map/pallas_call | solution.py:276
  103.6 4.5 %collective-permute-done.13.refs_1_ = bf16[1,512,512]{2,1,0:T(8,128)(2,1)S(1)} collective-permute-done((bf16[1,512,512]{2,1,0:T(8,128)(2,1)S(1)}, bf16[1,512,512]{2,1,0:T(8,128)(2,1)S(1)}, u32[]{:S(2)}, u32[]{:S(2)}) %collective-permute-start.13) | collective-permute-done | bytes 524320 | tf_op jit(solution)/shard_map/ppermute | solution.py:236
  108.1 3.7 %shard_map.71 = (bf16[13,512,512]{2,1,0:T(8,128)(2,1)S(1)}, f32[6,512,512]{2,1,0:T(8,128)S(1)}) custom-call(s32[6347]{0:T(1024)S(4)} %get-tuple-element.49.table, bf16[9,512,512]{2,1,0:T(8,128)(2,1)S(1)} %bitcast.12, bf16[1,512,512]{2,1,0:T(8,128)(2,1)S(1)} %shard_map.61.refs_0_, ...), custom_call_target="tpu_custom_call", output_to_operand_aliasing={{0}: (4, {}), {1}: (5, {})} | custom-call | flops 2684354560 | bytes 1048576 | tf_op jit(solution)/shard_map/pallas_call | solution.py:276
  111.8 1.6 %shard_map.72 = (bf16[13,512,512]{2,1,0:T(8,128)(2,1)S(1)}, f32[6,512,512]{2,1,0:T(8,128)S(1)}, bf16[1,512,512]{2,1,0:T(8,128)(2,1)S(1)}) custom-call(s32[6347]{0:T(1024)S(4)} %get-tuple-element.49.table, bf16[9,512,512]{2,1,0:T(8,128)(2,1)S(1)} %bitcast.12, ...), custom_call_target="tpu_custom_call", output_to_operand_aliasing={{0}: (6, {}), {1}: (7, {})} | custom-call | flops 2684354560 | bytes 1048576 | tf_op jit(solution)/shard_map/pallas_call | solution.py:276
  113.4 1.5 %shard_map.73 = (bf16[13,512,512]{2,1,0:T(8,128)(2,1)S(1)}, f32[6,512,512]{2,1,0:T(8,128)S(1)}, bf16[1,512,512]{2,1,0:T(8,128)(2,1)S(1)}) custom-call(s32[6347]{0:T(1024)S(4)} %get-tuple-element.49.table, bf16[9,512,512]{2,1,0:T(8,128)(2,1)S(1)} %bitcast.12, ...), custom_call_target="tpu_custom_call", output_to_operand_aliasing={{0}: (2, {}), {1}: (3, {})} | custom-call | flops 1073741824 | bytes 1048576 | tf_op jit(solution)/shard_map/pallas_call | solution.py:276
  115.0 2.0 %collective-permute-start.28 = (bf16[1,512,512]{2,1,0:T(8,128)(2,1)S(1)}, bf16[1,512,512]{2,1,0:T(8,128)(2,1)S(1)}, u32[]{:S(2)}, u32[]{:S(2)}) collective-permute-start(bf16[1,512,512]{2,1,0:T(8,128)(2,1)S(1)} %get-tuple-element.82), channel_id=1, source_target_pairs={{0,8},{1,17},{2,10},{3,19},{4,12},{5,21},{6,14},{7,23},{8,0},{9,25... | collective-permute-start | bytes 1572872 | tf_op jit(solution)/shard_map/ppermute | solution.py:236
  117.0 1.7 %shard_map.74 = (bf16[13,512,512]{2,1,0:T(8,128)(2,1)S(1)}, f32[6,512,512]{2,1,0:T(8,128)S(1)}, bf16[1,512,512]{2,1,0:T(8,128)(2,1)S(1)}) custom-call(s32[6347]{0:T(1024)S(4)} %get-tuple-element.49.table, bf16[9,512,512]{2,1,0:T(8,128)(2,1)S(1)} %bitcast.12, ...), custom_call_target="tpu_custom_call", output_to_operand_aliasing={{0}: (2, {}), {1}: (3, {})} | custom-call | flops 1073741824 | bytes 1048576 | tf_op jit(solution)/shard_map/pallas_call | solution.py:276
  118.8 2.2 %shard_map.75 = (bf16[13,512,512]{2,1,0:T(8,128)(2,1)S(1)}, f32[6,512,512]{2,1,0:T(8,128)S(1)}) custom-call(s32[6347]{0:T(1024)S(4)} %get-tuple-element.49.table, bf16[9,512,512]{2,1,0:T(8,128)(2,1)S(1)} %bitcast.12, bf16[13,512,512]{2,1,0:T(8,128)(2,1)S(1)} %get-tuple-element.84.refs_0_, ...), custom_call_target="tpu_custom_call", output_to_operand_aliasing={{0}: (2, {}), {1}: (3, {})} | custom-call | flops 2684354560 | bytes 1048576 | tf_op jit(solution)/shard_map/pallas_call | solution.py:276
  121.1 5.8 %shard_map.76 = (f32[6,512,512]{2,1,0:T(8,128)S(1)}, f32[3,1,2,512,512]{4,3,2,1,0:T(8,128)}) custom-call(s32[6347]{0:T(1024)S(4)} %get-tuple-element.49.table, s32[1]{0:T(128)} %bitcast.7.part_ref, bf16[9,512,512]{2,1,0:T(8,128)(2,1)S(1)} %bitcast.12, bf16[13,512,512]{2,1,0:T(8,128)(2,1)S(1)} %get-tuple-element.86.blocks, ...), custom_call_target="tpu_custom_call", output_to_operand_aliasing={{0}: (4, {})} | custom-call | flops 1048576 | bytes 1048576 | tf_op jit(solution)/shard_map/pallas_call | solution.py:276
  126.9 2.9 %collective-permute-done.28.refs_0_ = bf16[1,512,512]{2,1,0:T(8,128)(2,1)S(1)} collective-permute-done((bf16[1,512,512]{2,1,0:T(8,128)(2,1)S(1)}, bf16[1,512,512]{2,1,0:T(8,128)(2,1)S(1)}, u32[]{:S(2)}, u32[]{:S(2)}) %collective-permute-start.28) | collective-permute-done | bytes 524320 | tf_op jit(solution)/shard_map/ppermute | solution.py:236
  129.7 1.4 %shard_map.77.refs_1_ = f32[3,1,2,512,512]{4,3,2,1,0:T(8,128)} custom-call(s32[1]{0:T(128)} %bitcast.part_ref, bf16[1,512,512]{2,1,0:T(8,128)(2,1)S(1)} %collective-permute-done.28.refs_0_, bf16[1,512,512]{2,1,0:T(8,128)(2,1)S(1)} %collective-permute-done.29.refs_1_, f32[3,1,2,512,512]{4,3,2,1,0:T(8,128)} %get-tuple-element.88.refs_2_), custom_call_target="tpu_custom_call", output_to_operand_aliasing={{}: (3, {})} | custom-call | flops 1048576 | bytes 1048576 | tf_op jit(solution)/shard_map/pallas_call | solution.py:276
  131.2 4.2 %collective-permute-done.27.refs_0_ = bf16[1,512,512]{2,1,0:T(8,128)(2,1)S(1)} collective-permute-done((bf16[1,512,512]{2,1,0:T(8,128)(2,1)S(1)}, bf16[1,512,512]{2,1,0:T(8,128)(2,1)S(1)}, u32[]{:S(2)}, u32[]{:S(2)}) %collective-permute-start.27) | collective-permute-done | bytes 524320 | tf_op jit(solution)/shard_map/ppermute | solution.py:236
  135.4 1.1 shard_map.78
  (52 shorter events, 2.7 us)
Async XLA Ops:
  0.9 0.7 copy-start
  1.5 10.8 %copy-start.1 = (s32[3]{0:T(128)S(1)}, s32[3]{0:T(128)}, u32[]{:S(2)}) copy-start(s32[3]{0:T(128)} %shift.1) | copy-start | bytes 40
  5.9 9.0 %copy-start.2 = (s32[3,12]{1,0:T(4,128)S(1)}, s32[3,12]{1,0:T(4,128)}, u32[]{:S(2)}) copy-start(s32[3,12]{1,0:T(4,128)} %param.6) | copy-start | bytes 436
  5.9 6.5 %collective-permute-start.1 = (bf16[6,512,512]{2,1,0:T(8,128)(2,1)S(1)}, bf16[6,512,512]{2,1,0:T(8,128)(2,1)S(1)}, u32[]{:S(2)}, u32[]{:S(2)}) collective-permute-start(bf16[6,512,512]{2,1,0:T(8,128)(2,1)S(1)} %get-tuple-element.53), channel_id=1, source_target_pairs={{0,1},{1,0},{2,3},{3,2},{4,5},{5,4},{6,7},{7,6},{8,9},{9,8},{10,11... | collective-permute-start | bytes 9437192 | tf_op jit(solution)/shard_map/ppermute | solution.py:236
  8.3 13.0 %collective-permute-start.25 = (bf16[1,512,512]{2,1,0:T(8,128)(2,1)S(1)}, bf16[1,512,512]{2,1,0:T(8,128)(2,1)S(1)}, u32[]{:S(2)}, u32[]{:S(2)}) collective-permute-start(bf16[1,512,512]{2,1,0:T(8,128)(2,1)S(1)} %shard_map.57.refs_0_), channel_id=1, source_target_pairs={{0,1},{1,3},{2,0},{3,5},{4,2},{5,7},{6,4},{7,6},{8,9},{9,11},{10,8... | collective-permute-start | bytes 1572872 | tf_op jit(solution)/shard_map/ppermute | solution.py:236
  8.3 15.6 %collective-permute-start.22 = (bf16[1,512,512]{2,1,0:T(8,128)(2,1)S(1)}, bf16[1,512,512]{2,1,0:T(8,128)(2,1)S(1)}, u32[]{:S(2)}, u32[]{:S(2)}) collective-permute-start(bf16[1,512,512]{2,1,0:T(8,128)(2,1)S(1)} %get-tuple-element.54.refs_1_), channel_id=1, source_target_pairs={{0,1},{1,3},{2,0},{3,5},{4,2},{5,7},{6,4},{7,6},{8,9},{9,11},{10,8... | collective-permute-start | bytes 1572872 | tf_op jit(solution)/shard_map/ppermute | solution.py:236
  11.1 23.8 %collective-permute-start.19 = (bf16[1,512,512]{2,1,0:T(8,128)(2,1)S(1)}, bf16[1,512,512]{2,1,0:T(8,128)(2,1)S(1)}, u32[]{:S(2)}, u32[]{:S(2)}) collective-permute-start(bf16[1,512,512]{2,1,0:T(8,128)(2,1)S(1)} %get-tuple-element.55.refs_2_), channel_id=1, source_target_pairs={{0,1},{1,3},{2,0},{3,5},{4,2},{5,7},{6,4},{7,6},{8,9},{9,11},{10,8... | collective-permute-start | bytes 1572872 | tf_op jit(solution)/shard_map/ppermute | solution.py:236
  12.4 71.7 %slice-start = ((s8[4718592]{0:T(1024)(128)(4,1)}), s8[4194304]{0:T(1024)(128)(4,1)S(1)}, s32[]{:S(2)}) async-start(s8[4718592]{0:T(1024)(128)(4,1)} %bitcast.11), calls=%async_computation | async-start | bytes 8388608
  12.7 24.2 %collective-permute-start.5 = (bf16[1,256,512]{2,1,0:T(8,128)(2,1)S(1)}, bf16[1,256,512]{2,1,0:T(8,128)(2,1)S(1)}, u32[]{:S(2)}, u32[]{:S(2)}) collective-permute-start(bf16[1,256,512]{2,1,0:T(8,128)(2,1)S(1)} %get-tuple-element.58), channel_id=1, source_target_pairs={{0,8},{1,17},{2,10},{3,19},{4,12},{5,21},{6,14},{7,23},{8,0},{9,25... | collective-permute-start | bytes 786440 | tf_op jit(solution)/shard_map/ppermute | solution.py:236
  15.0 4.3 %collective-permute-start = (s32[3,12]{1,0:T(4,128)S(1)}, s32[3,12]{1,0:T(4,128)S(1)}, u32[]{:S(2)}, u32[]{:S(2)}) collective-permute-start(s32[3,12]{1,0:T(4,128)S(1)} %broadcast_add_fusion.own_ref), channel_id=1, source_target_pairs={{0,8},{1,17},{2,10},{3,19},{4,12},{5,21},{6,14},{7,23},{8,0},{9,25... | collective-permute-start | bytes 440 | tf_op jit(solution)/shard_map/ppermute | solution.py:236
  19.3 19.2 %collective-permute-start.2 = (bf16[1,256,512]{2,1,0:T(8,128)(2,1)S(1)}, bf16[1,256,512]{2,1,0:T(8,128)(2,1)S(1)}, u32[]{:S(2)}, u32[]{:S(2)}) collective-permute-start(bf16[1,256,512]{2,1,0:T(8,128)(2,1)S(1)} %get-tuple-element.57), channel_id=1, source_target_pairs={{0,8},{1,17},{2,10},{3,19},{4,12},{5,21},{6,14},{7,23},{8,0},{9,25... | collective-permute-start | bytes 786440 | tf_op jit(solution)/shard_map/ppermute | solution.py:236
  21.3 18.7 %collective-permute-start.24 = (bf16[1,512,512]{2,1,0:T(8,128)(2,1)S(1)}, bf16[1,512,512]{2,1,0:T(8,128)(2,1)S(1)}, u32[]{:S(2)}, u32[]{:S(2)}) collective-permute-start(bf16[1,512,512]{2,1,0:T(8,128)(2,1)S(1)} %get-tuple-element.64.chosen), channel_id=1, source_target_pairs={{0,2},{1,0},{2,4},{3,1},{4,6},{5,3},{6,7},{7,5},{8,10},{9,8},{10,1... | collective-permute-start | bytes 1572872 | tf_op jit(solution)/shard_map/ppermute | solution.py:236
  23.8 16.2 %collective-permute-start.14 = (bf16[1,512,512]{2,1,0:T(8,128)(2,1)S(1)}, bf16[1,512,512]{2,1,0:T(8,128)(2,1)S(1)}, u32[]{:S(2)}, u32[]{:S(2)}) collective-permute-start(bf16[1,512,512]{2,1,0:T(8,128)(2,1)S(1)} %get-tuple-element.60), channel_id=1, source_target_pairs={{0,8},{1,17},{2,10},{3,19},{4,12},{5,21},{6,14},{7,23},{8,0},{9,25... | collective-permute-start | bytes 1572872 | tf_op jit(solution)/shard_map/ppermute | solution.py:236
  34.9 8.7 %collective-permute-start.21 = (bf16[1,512,512]{2,1,0:T(8,128)(2,1)S(1)}, bf16[1,512,512]{2,1,0:T(8,128)(2,1)S(1)}, u32[]{:S(2)}, u32[]{:S(2)}) collective-permute-start(bf16[1,512,512]{2,1,0:T(8,128)(2,1)S(1)} %get-tuple-element.63.chosen), channel_id=1, source_target_pairs={{0,2},{1,0},{2,4},{3,1},{4,6},{5,3},{6,7},{7,5},{8,10},{9,8},{10,1... | collective-permute-start | bytes 1572872 | tf_op jit(solution)/shard_map/ppermute | solution.py:236
  36.9 17.8 %collective-permute-start.18 = (bf16[1,512,512]{2,1,0:T(8,128)(2,1)S(1)}, bf16[1,512,512]{2,1,0:T(8,128)(2,1)S(1)}, u32[]{:S(2)}, u32[]{:S(2)}) collective-permute-start(bf16[1,512,512]{2,1,0:T(8,128)(2,1)S(1)} %get-tuple-element.62.chosen), channel_id=1, source_target_pairs={{0,2},{1,0},{2,4},{3,1},{4,6},{5,3},{6,7},{7,5},{8,10},{9,8},{10,1... | collective-permute-start | bytes 1572872 | tf_op jit(solution)/shard_map/ppermute | solution.py:236
  38.5 16.2 %collective-permute-start.10 = (bf16[1,512,512]{2,1,0:T(8,128)(2,1)S(1)}, bf16[1,512,512]{2,1,0:T(8,128)(2,1)S(1)}, u32[]{:S(2)}, u32[]{:S(2)}) collective-permute-start(bf16[1,512,512]{2,1,0:T(8,128)(2,1)S(1)} %get-tuple-element.59), channel_id=1, source_target_pairs={{0,8},{1,17},{2,10},{3,19},{4,12},{5,21},{6,14},{7,23},{8,0},{9,25... | collective-permute-start | bytes 1572872 | tf_op jit(solution)/shard_map/ppermute | solution.py:236
  40.0 20.4 %collective-permute-start.6 = (bf16[1,256,512]{2,1,0:T(8,128)(2,1)S(1)}, bf16[1,256,512]{2,1,0:T(8,128)(2,1)S(1)}, u32[]{:S(2)}, u32[]{:S(2)}) collective-permute-start(bf16[1,256,512]{2,1,0:T(8,128)(2,1)S(1)} %collective-permute-done.5.chosen), channel_id=1, source_target_pairs={{0,2},{1,0},{2,4},{3,1},{4,6},{5,3},{6,7},{7,5},{8,10},{9,8},{10,1... | collective-permute-start | bytes 786440 | tf_op jit(solution)/shard_map/ppermute | solution.py:236
  40.0 36.3 %collective-permute-start.15 = (bf16[1,512,512]{2,1,0:T(8,128)(2,1)S(1)}, bf16[1,512,512]{2,1,0:T(8,128)(2,1)S(1)}, u32[]{:S(2)}, u32[]{:S(2)}) collective-permute-start(bf16[1,512,512]{2,1,0:T(8,128)(2,1)S(1)} %collective-permute-done.14.chosen), channel_id=1, source_target_pairs={{0,2},{1,0},{2,4},{3,1},{4,6},{5,3},{6,7},{7,5},{8,10},{9,8},{10,1... | collective-permute-start | bytes 1572872 | tf_op jit(solution)/shard_map/ppermute | solution.py:236
  43.6 17.0 %collective-permute-start.7 = (bf16[1,256,512]{2,1,0:T(8,128)(2,1)S(1)}, bf16[1,256,512]{2,1,0:T(8,128)(2,1)S(1)}, u32[]{:S(2)}, u32[]{:S(2)}) collective-permute-start(bf16[1,256,512]{2,1,0:T(8,128)(2,1)S(1)} %collective-permute-done.5.chosen), channel_id=1, source_target_pairs={{0,1},{1,3},{2,0},{3,5},{4,2},{5,7},{6,4},{7,6},{8,9},{9,11},{10,8... | collective-permute-start | bytes 786440 | tf_op jit(solution)/shard_map/ppermute | solution.py:236
  54.7 23.6 %collective-permute-start.16 = (bf16[1,512,512]{2,1,0:T(8,128)(2,1)S(1)}, bf16[1,512,512]{2,1,0:T(8,128)(2,1)S(1)}, u32[]{:S(2)}, u32[]{:S(2)}) collective-permute-start(bf16[1,512,512]{2,1,0:T(8,128)(2,1)S(1)} %collective-permute-done.14.chosen), channel_id=1, source_target_pairs={{0,1},{1,3},{2,0},{3,5},{4,2},{5,7},{6,4},{7,6},{8,9},{9,11},{10,8... | collective-permute-start | bytes 1572872 | tf_op jit(solution)/shard_map/ppermute | solution.py:236
  54.7 17.0 %collective-permute-start.3 = (bf16[1,256,512]{2,1,0:T(8,128)(2,1)S(1)}, bf16[1,256,512]{2,1,0:T(8,128)(2,1)S(1)}, u32[]{:S(2)}, u32[]{:S(2)}) collective-permute-start(bf16[1,256,512]{2,1,0:T(8,128)(2,1)S(1)} %collective-permute-done.2.chosen), channel_id=1, source_target_pairs={{0,2},{1,0},{2,4},{3,1},{4,6},{5,3},{6,7},{7,5},{8,10},{9,8},{10,1... | collective-permute-start | bytes 786440 | tf_op jit(solution)/shard_map/ppermute | solution.py:236
  60.3 15.7 %collective-permute-start.4 = (bf16[1,256,512]{2,1,0:T(8,128)(2,1)S(1)}, bf16[1,256,512]{2,1,0:T(8,128)(2,1)S(1)}, u32[]{:S(2)}, u32[]{:S(2)}) collective-permute-start(bf16[1,256,512]{2,1,0:T(8,128)(2,1)S(1)} %collective-permute-done.2.chosen), channel_id=1, source_target_pairs={{0,1},{1,3},{2,0},{3,5},{4,2},{5,7},{6,4},{7,6},{8,9},{9,11},{10,8... | collective-permute-start | bytes 786440 | tf_op jit(solution)/shard_map/ppermute | solution.py:236
  60.3 23.8 %slice-start.1 = ((s8[4718592]{0:T(1024)(128)(4,1)}), s8[524288]{0:T(1024)(128)(4,1)S(1)}, s32[]{:S(2)}) async-start(s8[4718592]{0:T(1024)(128)(4,1)} %bitcast.11), calls=%async_computation.1 | async-start | bytes 1048576
  60.6 21.9 %collective-permute-start.26 = (bf16[1,512,512]{2,1,0:T(8,128)(2,1)S(1)}, bf16[1,512,512]{2,1,0:T(8,128)(2,1)S(1)}, u32[]{:S(2)}, u32[]{:S(2)}) collective-permute-start(bf16[1,512,512]{2,1,0:T(8,128)(2,1)S(1)} %shard_map.65.refs_0_), channel_id=1, source_target_pairs={{0,16},{1,9},{2,18},{3,11},{4,20},{5,13},{6,22},{7,15},{8,24},{9,1... | collective-permute-start | bytes 1572872 | tf_op jit(solution)/shard_map/ppermute | solution.py:236
  71.7 15.7 %collective-permute-start.11 = (bf16[1,512,512]{2,1,0:T(8,128)(2,1)S(1)}, bf16[1,512,512]{2,1,0:T(8,128)(2,1)S(1)}, u32[]{:S(2)}, u32[]{:S(2)}) collective-permute-start(bf16[1,512,512]{2,1,0:T(8,128)(2,1)S(1)} %collective-permute-done.10.chosen), channel_id=1, source_target_pairs={{0,2},{1,0},{2,4},{3,1},{4,6},{5,3},{6,7},{7,5},{8,10},{9,8},{10,1... | collective-permute-start | bytes 1572872 | tf_op jit(solution)/shard_map/ppermute | solution.py:236
  76.0 11.5 %collective-permute-start.12 = (bf16[1,512,512]{2,1,0:T(8,128)(2,1)S(1)}, bf16[1,512,512]{2,1,0:T(8,128)(2,1)S(1)}, u32[]{:S(2)}, u32[]{:S(2)}) collective-permute-start(bf16[1,512,512]{2,1,0:T(8,128)(2,1)S(1)} %collective-permute-done.10.chosen), channel_id=1, source_target_pairs={{0,1},{1,3},{2,0},{3,5},{4,2},{5,7},{6,4},{7,6},{8,9},{9,11},{10,8... | collective-permute-start | bytes 1572872 | tf_op jit(solution)/shard_map/ppermute | solution.py:236
  76.4 13.5 %collective-permute-start.23 = (bf16[1,512,512]{2,1,0:T(8,128)(2,1)S(1)}, bf16[1,512,512]{2,1,0:T(8,128)(2,1)S(1)}, u32[]{:S(2)}, u32[]{:S(2)}) collective-permute-start(bf16[1,512,512]{2,1,0:T(8,128)(2,1)S(1)} %shard_map.64.refs_0_), channel_id=1, source_target_pairs={{0,16},{1,9},{2,18},{3,11},{4,20},{5,13},{6,22},{7,15},{8,24},{9,1... | collective-permute-start | bytes 1572872 | tf_op jit(solution)/shard_map/ppermute | solution.py:236
  78.3 14.6 %collective-permute-start.20 = (bf16[1,512,512]{2,1,0:T(8,128)(2,1)S(1)}, bf16[1,512,512]{2,1,0:T(8,128)(2,1)S(1)}, u32[]{:S(2)}, u32[]{:S(2)}) collective-permute-start(bf16[1,512,512]{2,1,0:T(8,128)(2,1)S(1)} %shard_map.63.refs_0_), channel_id=1, source_target_pairs={{0,16},{1,9},{2,18},{3,11},{4,20},{5,13},{6,22},{7,15},{8,24},{9,1... | collective-permute-start | bytes 1572872 | tf_op jit(solution)/shard_map/ppermute | solution.py:236
  82.5 14.3 %collective-permute-start.17 = (bf16[1,512,512]{2,1,0:T(8,128)(2,1)S(1)}, bf16[1,512,512]{2,1,0:T(8,128)(2,1)S(1)}, u32[]{:S(2)}, u32[]{:S(2)}) collective-permute-start(bf16[1,512,512]{2,1,0:T(8,128)(2,1)S(1)} %shard_map.62.refs_0_), channel_id=1, source_target_pairs={{0,16},{1,9},{2,18},{3,11},{4,20},{5,13},{6,22},{7,15},{8,24},{9,1... | collective-permute-start | bytes 1572872 | tf_op jit(solution)/shard_map/ppermute | solution.py:236
  87.4 24.4 %collective-permute-start.9 = (bf16[1,256,512]{2,1,0:T(8,128)(2,1)S(1)}, bf16[1,256,512]{2,1,0:T(8,128)(2,1)S(1)}, u32[]{:S(2)}, u32[]{:S(2)}) collective-permute-start(bf16[1,256,512]{2,1,0:T(8,128)(2,1)S(1)} %shard_map.60.refs_1_), channel_id=1, source_target_pairs={{0,16},{1,9},{2,18},{3,11},{4,20},{5,13},{6,22},{7,15},{8,24},{9,1... | collective-permute-start | bytes 786440 | tf_op jit(solution)/shard_map/ppermute | solution.py:236
  87.5 24.3 %collective-permute-start.8 = (bf16[1,256,512]{2,1,0:T(8,128)(2,1)S(1)}, bf16[1,256,512]{2,1,0:T(8,128)(2,1)S(1)}, u32[]{:S(2)}, u32[]{:S(2)}) collective-permute-start(bf16[1,256,512]{2,1,0:T(8,128)(2,1)S(1)} %shard_map.59.refs_0_), channel_id=1, source_target_pairs={{0,16},{1,9},{2,18},{3,11},{4,20},{5,13},{6,22},{7,15},{8,24},{9,1... | collective-permute-start | bytes 786440 | tf_op jit(solution)/shard_map/ppermute | solution.py:236
  89.8 18.3 %collective-permute-start.13 = (bf16[1,512,512]{2,1,0:T(8,128)(2,1)S(1)}, bf16[1,512,512]{2,1,0:T(8,128)(2,1)S(1)}, u32[]{:S(2)}, u32[]{:S(2)}) collective-permute-start(bf16[1,512,512]{2,1,0:T(8,128)(2,1)S(1)} %shard_map.61.refs_0_), channel_id=1, source_target_pairs={{0,16},{1,9},{2,18},{3,11},{4,20},{5,13},{6,22},{7,15},{8,24},{9,1... | collective-permute-start | bytes 1572872 | tf_op jit(solution)/shard_map/ppermute | solution.py:236
  114.9 12.0 %collective-permute-start.29 = (bf16[1,512,512]{2,1,0:T(8,128)(2,1)S(1)}, bf16[1,512,512]{2,1,0:T(8,128)(2,1)S(1)}, u32[]{:S(2)}, u32[]{:S(2)}) collective-permute-start(bf16[1,512,512]{2,1,0:T(8,128)(2,1)S(1)} %get-tuple-element.83), channel_id=1, source_target_pairs={{0,8},{1,17},{2,10},{3,19},{4,12},{5,21},{6,14},{7,23},{8,0},{9,25... | collective-permute-start | bytes 1572872 | tf_op jit(solution)/shard_map/ppermute | solution.py:236
  115.0 14.8 %collective-permute-start.28 = (bf16[1,512,512]{2,1,0:T(8,128)(2,1)S(1)}, bf16[1,512,512]{2,1,0:T(8,128)(2,1)S(1)}, u32[]{:S(2)}, u32[]{:S(2)}) collective-permute-start(bf16[1,512,512]{2,1,0:T(8,128)(2,1)S(1)} %get-tuple-element.82), channel_id=1, source_target_pairs={{0,8},{1,17},{2,10},{3,19},{4,12},{5,21},{6,14},{7,23},{8,0},{9,25... | collective-permute-start | bytes 1572872 | tf_op jit(solution)/shard_map/ppermute | solution.py:236
  118.7 16.7 %collective-permute-start.27 = (bf16[1,512,512]{2,1,0:T(8,128)(2,1)S(1)}, bf16[1,512,512]{2,1,0:T(8,128)(2,1)S(1)}, u32[]{:S(2)}, u32[]{:S(2)}) collective-permute-start(bf16[1,512,512]{2,1,0:T(8,128)(2,1)S(1)} %get-tuple-element.81), channel_id=1, source_target_pairs={{0,8},{1,17},{2,10},{3,19},{4,12},{5,21},{6,14},{7,23},{8,0},{9,25... | collective-permute-start | bytes 1572872 | tf_op jit(solution)/shard_map/ppermute | solution.py:236

commit v3 on v1

--- a/solution.py
+++ b/solution.py
@@ -73,11 +73,13 @@
             def one_job(j, _):
                 first = index * slots + j * MEMBERS
                 upto = jnp.minimum(MEMBERS, have - j * MEMBERS)
-                stage = lax.div(member[first + upto - 1], ways)
                 last = 2 * local - 1
-                call = jnp.where(stage == last, last + 1 + min(k, local), stage)
-                if k >= local:
-                    call = jnp.where(stage == last - 1, last, call)
+                latest = member[first + upto - 1]
+                stage = jnp.where(latest == last * ways, last - 1, lax.div(latest, ways))
+                if k < local:
+                    call = jnp.where(stage == last, last + k, stage)
+                else:
+                    call = jnp.where(stage < last - 2, stage, last + local)
                 place = filled[call]
                 filled[call] = place + 1
                 table[call] = place + 1
@@ -173,7 +175,7 @@
         done = done + count * size
 
 
-def stage_kernel(call, calls, base, ways, arrived, sends, scale, table, coupling, *refs):
+def stage_kernel(call, calls, layout, arrived, sends, scale, table, coupling, *refs):
     parts = refs[:arrived]
     first_call = call == 0
     refs = refs[arrived:] if first_call else refs[arrived + 2 :]
@@ -183,13 +185,14 @@
     if first_call:
         blocks[slots] = jnp.zeros(blocks.shape[1:], blocks.dtype)
         total[...] = jnp.zeros(total.shape, total.dtype)
-    for way in range(ways if arrived else 0):
+    parts = list(parts)
+    for slot, cuts in layout:
         top = 0
-        for part in parts[way * arrived // ways : (way + 1) * arrived // ways]:
-            rows = part.shape[1]
-            blocks[base + way, top : top + rows] = part[0]
-            top += rows
-    run_jobs(call, calls, table, coupling, blocks, total)
+        for _ in range(cuts):
+            part = parts.pop(0)
+            blocks[slot, top : top + part.shape[1]] = part[0]
+            top += part.shape[1]
+    run_jobs(call, calls, table, coupling, blocks, total, wide=len(layout) > 2)
     if send is not None:
         for i, k in enumerate(sends):
             send[i] = (total[k] * scale).astype(send.dtype)
@@ -257,7 +260,7 @@
         ways = 1 << bits
         slots = 2 * local * ways
         last = 2 * local - 1
-        calls = last + local + 2
+        calls = last + local + 1
         low = jnp.bfloat16
         scale = 1.0 / momenta
         m, e = lax.axis_index("mom"), lax.axis_index("en")
@@ -400,10 +403,10 @@
             pltpu.VMEM((2 * local, *block_shape), jnp.float32),
         ]
 
-        def stage(call, arrived, state, sends, jobs, base=0):
+        def stage(call, arrived, state, sends, jobs, layout=()):
             given = [] if state is None else list(state)
             result = kernel(
-                functools.partial(stage_kernel, call, calls, base, ways, len(arrived), sends, scale),
+                functools.partial(stage_kernel, call, calls, layout, len(arrived), sends, scale),
                 table,
                 weights,
                 *arrived,
@@ -424,15 +427,19 @@
             for bit in range(bits):
                 for values in list(arrived):
                     arrived.append(sends(values, gather_bit(bit)))
+            places = [call * ways + way for way in range(ways)]
+            if call == last - 1:
+                arrived, places = [*arrived, stages[last]], [*places, last * ways]
+            if call == last:
+                arrived, places = arrived[1:], places[1:]
+            layout = [(place, len(values)) for place, values in zip(places, arrived)]
             arrived = [piece for values in arrived for piece in values]
             sends_now = [0] if call == last else []
-            state, sent = stage(call + (call == last), arrived, state, sends_now, 5, call * ways)
-        got = []
+            state, sent = stage(call, arrived, state, sends_now, 5, layout)
         for k in range(local):
             if k:
-                state, sent = stage(last + 1 + k, [], state, [k], 2)
+                state, sent = stage(last + k, [], state, [k], 2)
             got.append(send(sent[0], partner))
-        state, _ = stage(last, [], state, [], 5)
 
         hbm = pl.BlockSpec(memory_space=pltpu.HBM)
         out_shape = jax.ShapeDtypeStruct(green_blocks.shape, jnp.float32)
@@ -441,7 +448,7 @@
             pltpu.SemaphoreType.DMA((local,)),
         ]
         _, result = kernel(
-            functools.partial(finish_kernel, last + 1 + local, calls, scale),
+            functools.partial(finish_kernel, last + local, calls, scale),
             table,
             mine.reshape(1),
             weights,

time: 138 us -> 139 us (level)
  waiting for transfers between devices: 53.6 us -> 55.2 us
    ppermute x30, waiting for transfers between devices: 53.6 us -> 55.2 us  [move(): return lax.ppermute(value, both, pairs)]
    pallas_call x23 -> x22, Pallas kernels: 45.3 us -> 44.1 us  [kernel(): pl.pallas_call(act, compiler_params=pltpu.CompilerParams(vmem_limit_bytes...]
where the time goes in v3:
time: 139 us; the launch traced here: 137 us
  waiting for transfers between devices  55.2 us (40%)
  Pallas kernels  44.1 us (32%)
  starting transfers between devices  35.6 us (26%)
    ppermute x30, waiting for transfers between devices, move(): return lax.ppermute(value, both, pairs)  55.2 us
    pallas_call x22, Pallas kernels, kernel(): pl.pallas_call(act, compiler_params=pltpu.CompilerParams(vmem_limit_bytes...  44.1 us
    ppermute x30, starting transfers between devices, move(): return lax.ppermute(value, both, pairs)  35.6 us
  transfers between devices with their start and end apart: 30, of which 11 were waited for; matrix products, arithmetic and copies ran while one was open for 0% of the time, Pallas kernels for 27%

profile of v3, /device:TPU:0, one launch (start us, length us, event | category | flops | bytes accessed | tf_op | source)
XLA Modules:
  0.0 137.0 jit_solution(9208645993068628597)
XLA Ops:
  0.9 0.6 copy-done
  1.5 4.3 %shard_map.56 = (bf16[1,512,512]{2,1,0:T(8,128)(2,1)S(1)}, bf16[1,512,512]{2,1,0:T(8,128)(2,1)S(1)}, bf16[3,512,512]{2,1,0:T(8,128)(2,1)S(1)}, bf16[6,512,512]{2...) custom-call(s32[4]{0:T(128)S(1)} %pad_add_fusion.1.part_ref, s32[3]{0:T(128)S(1)} %copy-done, f32[1]{0:T(128)S(6)} %copy.40.occupancy, ...), custom_call_target="tpu_custom_call" | custom-call | flops 1048576 | bytes 1048576 | tf_op jit(solution)/shard_map/pallas_call | solution.py:279
  5.9 0.6 collective-permute-start.1
  6.4 1.8 %shard_map.57.refs_0_ = bf16[1,512,512]{2,1,0:T(8,128)(2,1)S(1)} custom-call(s32[4]{0:T(128)S(1)} %pad_add_fusion.1.part_ref, f32[3,2,512,512]{3,2,1,0:T(8,128)} %bitcast.14), custom_call_target="tpu_custom_call" | custom-call | flops 1048576 | bytes 1048576 | tf_op jit(solution)/shard_map/pallas_call | solution.py:279
  8.3 2.8 %collective-permute-start.22 = (bf16[1,512,512]{2,1,0:T(8,128)(2,1)S(1)}, bf16[1,512,512]{2,1,0:T(8,128)(2,1)S(1)}, u32[]{:S(2)}, u32[]{:S(2)}) collective-permute-start(bf16[1,512,512]{2,1,0:T(8,128)(2,1)S(1)} %get-tuple-element.50.refs_1_), channel_id=1, source_target_pairs={{0,1},{1,3},{2,0},{3,5},{4,2},{5,7},{6,4},{7,6},{8,9},{9,11},{10,8... | collective-permute-start | bytes 1572872 | tf_op jit(solution)/shard_map/ppermute | solution.py:239
  11.1 1.3 collective-permute-start.19
  12.7 2.2 %collective-permute-start.6 = (bf16[1,256,512]{2,1,0:T(8,128)(2,1)S(1)}, bf16[1,256,512]{2,1,0:T(8,128)(2,1)S(1)}, u32[]{:S(2)}, u32[]{:S(2)}) collective-permute-start(bf16[1,256,512]{2,1,0:T(8,128)(2,1)S(1)} %get-tuple-element.54), channel_id=1, source_target_pairs={{0,8},{1,17},{2,10},{3,19},{4,12},{5,21},{6,14},{7,23},{8,0},{9,25... | collective-permute-start | bytes 786440 | tf_op jit(solution)/shard_map/ppermute | solution.py:239
  15.0 4.3 %collective-permute-done.partner_ref = s32[3,12]{1,0:T(4,128)S(1)} collective-permute-done((s32[3,12]{1,0:T(4,128)S(1)}, s32[3,12]{1,0:T(4,128)S(1)}, u32[]{:S(2)}, u32[]{:S(2)}) %collective-permute-start) | collective-permute-done | bytes 176 | tf_op jit(solution)/shard_map/ppermute | solution.py:239
  19.3 2.0 %collective-permute-start.2 = (bf16[1,256,512]{2,1,0:T(8,128)(2,1)S(1)}, bf16[1,256,512]{2,1,0:T(8,128)(2,1)S(1)}, u32[]{:S(2)}, u32[]{:S(2)}) collective-permute-start(bf16[1,256,512]{2,1,0:T(8,128)(2,1)S(1)} %get-tuple-element.53), channel_id=1, source_target_pairs={{0,8},{1,17},{2,10},{3,19},{4,12},{5,21},{6,14},{7,23},{8,0},{9,25... | collective-permute-start | bytes 786440 | tf_op jit(solution)/shard_map/ppermute | solution.py:239
  21.3 1.6 %collective-permute-start.24 = (bf16[1,512,512]{2,1,0:T(8,128)(2,1)S(1)}, bf16[1,512,512]{2,1,0:T(8,128)(2,1)S(1)}, u32[]{:S(2)}, u32[]{:S(2)}) collective-permute-start(bf16[1,512,512]{2,1,0:T(8,128)(2,1)S(1)} %get-tuple-element.60.chosen), channel_id=1, source_target_pairs={{0,2},{1,0},{2,4},{3,1},{4,6},{5,3},{6,7},{7,5},{8,10},{9,8},{10,1... | collective-permute-start | bytes 1572872 | tf_op jit(solution)/shard_map/ppermute | solution.py:239
  22.9 1.0 collective-permute-done.22.gone
  23.8 2.4 %collective-permute-start.14 = (bf16[1,512,512]{2,1,0:T(8,128)(2,1)S(1)}, bf16[1,512,512]{2,1,0:T(8,128)(2,1)S(1)}, u32[]{:S(2)}, u32[]{:S(2)}) collective-permute-start(bf16[1,512,512]{2,1,0:T(8,128)(2,1)S(1)} %get-tuple-element.56), channel_id=1, source_target_pairs={{0,8},{1,17},{2,10},{3,19},{4,12},{5,21},{6,14},{7,23},{8,0},{9,25... | collective-permute-start | bytes 1572872 | tf_op jit(solution)/shard_map/ppermute | solution.py:239
  26.2 8.6 %collective-permute-done.19.gone = bf16[1,512,512]{2,1,0:T(8,128)(2,1)S(1)} collective-permute-done((bf16[1,512,512]{2,1,0:T(8,128)(2,1)S(1)}, bf16[1,512,512]{2,1,0:T(8,128)(2,1)S(1)}, u32[]{:S(2)}, u32[]{:S(2)}) %collective-permute-start.19) | collective-permute-done | bytes 524320 | tf_op jit(solution)/shard_map/ppermute | solution.py:239
  34.9 2.0 %collective-permute-start.21 = (bf16[1,512,512]{2,1,0:T(8,128)(2,1)S(1)}, bf16[1,512,512]{2,1,0:T(8,128)(2,1)S(1)}, u32[]{:S(2)}, u32[]{:S(2)}) collective-permute-start(bf16[1,512,512]{2,1,0:T(8,128)(2,1)S(1)} %get-tuple-element.59.chosen), channel_id=1, source_target_pairs={{0,2},{1,0},{2,4},{3,1},{4,6},{5,3},{6,7},{7,5},{8,10},{9,8},{10,1... | collective-permute-start | bytes 1572872 | tf_op jit(solution)/shard_map/ppermute | solution.py:239
  36.9 1.6 %collective-permute-start.18 = (bf16[1,512,512]{2,1,0:T(8,128)(2,1)S(1)}, bf16[1,512,512]{2,1,0:T(8,128)(2,1)S(1)}, u32[]{:S(2)}, u32[]{:S(2)}) collective-permute-start(bf16[1,512,512]{2,1,0:T(8,128)(2,1)S(1)} %get-tuple-element.58.chosen), channel_id=1, source_target_pairs={{0,2},{1,0},{2,4},{3,1},{4,6},{5,3},{6,7},{7,5},{8,10},{9,8},{10,1... | collective-permute-start | bytes 1572872 | tf_op jit(solution)/shard_map/ppermute | solution.py:239
  38.5 1.5 %collective-permute-start.10 = (bf16[1,512,512]{2,1,0:T(8,128)(2,1)S(1)}, bf16[1,512,512]{2,1,0:T(8,128)(2,1)S(1)}, u32[]{:S(2)}, u32[]{:S(2)}) collective-permute-start(bf16[1,512,512]{2,1,0:T(8,128)(2,1)S(1)} %get-tuple-element.55), channel_id=1, source_target_pairs={{0,8},{1,17},{2,10},{3,19},{4,12},{5,21},{6,14},{7,23},{8,0},{9,25... | collective-permute-start | bytes 1572872 | tf_op jit(solution)/shard_map/ppermute | solution.py:239
  40.0 0.8 collective-permute-start.15
  40.9 2.7 %collective-permute-done.21.came = bf16[1,512,512]{2,1,0:T(8,128)(2,1)S(1)} collective-permute-done((bf16[1,512,512]{2,1,0:T(8,128)(2,1)S(1)}, bf16[1,512,512]{2,1,0:T(8,128)(2,1)S(1)}, u32[]{:S(2)}, u32[]{:S(2)}) %collective-permute-start.21) | collective-permute-done | bytes 524320 | tf_op jit(solution)/shard_map/ppermute | solution.py:239
  43.6 11.1 %collective-permute-done.18.came = bf16[1,512,512]{2,1,0:T(8,128)(2,1)S(1)} collective-permute-done((bf16[1,512,512]{2,1,0:T(8,128)(2,1)S(1)}, bf16[1,512,512]{2,1,0:T(8,128)(2,1)S(1)}, u32[]{:S(2)}, u32[]{:S(2)}) %collective-permute-start.18) | collective-permute-done | bytes 524320 | tf_op jit(solution)/shard_map/ppermute | solution.py:239
  54.7 2.5 %collective-permute-start.3 = (bf16[1,256,512]{2,1,0:T(8,128)(2,1)S(1)}, bf16[1,256,512]{2,1,0:T(8,128)(2,1)S(1)}, u32[]{:S(2)}, u32[]{:S(2)}) collective-permute-start(bf16[1,256,512]{2,1,0:T(8,128)(2,1)S(1)} %collective-permute-done.2.chosen), channel_id=1, source_target_pairs={{0,2},{1,0},{2,4},{3,1},{4,6},{5,3},{6,7},{7,5},{8,10},{9,8},{10,1... | collective-permute-start | bytes 786440 | tf_op jit(solution)/shard_map/ppermute | solution.py:239
  57.2 3.1 %collective-permute-done.7.came = bf16[1,256,512]{2,1,0:T(8,128)(2,1)S(1)} collective-permute-done((bf16[1,256,512]{2,1,0:T(8,128)(2,1)S(1)}, bf16[1,256,512]{2,1,0:T(8,128)(2,1)S(1)}, u32[]{:S(2)}, u32[]{:S(2)}) %collective-permute-start.7) | collective-permute-done | bytes 262176 | tf_op jit(solution)/shard_map/ppermute | solution.py:239
  60.3 0.3 shard_map.65.refs_0_
  60.6 1.6 %collective-permute-start.26 = (bf16[1,512,512]{2,1,0:T(8,128)(2,1)S(1)}, bf16[1,512,512]{2,1,0:T(8,128)(2,1)S(1)}, u32[]{:S(2)}, u32[]{:S(2)}) collective-permute-start(bf16[1,512,512]{2,1,0:T(8,128)(2,1)S(1)} %shard_map.65.refs_0_), channel_id=1, source_target_pairs={{0,16},{1,9},{2,18},{3,11},{4,20},{5,13},{6,22},{7,15},{8,24},{9,1... | collective-permute-start | bytes 1572872 | tf_op jit(solution)/shard_map/ppermute | solution.py:239
  62.2 9.5 %collective-permute-done.3.came = bf16[1,256,512]{2,1,0:T(8,128)(2,1)S(1)} collective-permute-done((bf16[1,256,512]{2,1,0:T(8,128)(2,1)S(1)}, bf16[1,256,512]{2,1,0:T(8,128)(2,1)S(1)}, u32[]{:S(2)}, u32[]{:S(2)}) %collective-permute-start.3) | collective-permute-done | bytes 262176 | tf_op jit(solution)/shard_map/ppermute | solution.py:239
  71.7 4.4 %collective-permute-start.11 = (bf16[1,512,512]{2,1,0:T(8,128)(2,1)S(1)}, bf16[1,512,512]{2,1,0:T(8,128)(2,1)S(1)}, u32[]{:S(2)}, u32[]{:S(2)}) collective-permute-start(bf16[1,512,512]{2,1,0:T(8,128)(2,1)S(1)} %collective-permute-done.10.chosen), channel_id=1, source_target_pairs={{0,2},{1,0},{2,4},{3,1},{4,6},{5,3},{6,7},{7,5},{8,10},{9,8},{10,1... | collective-permute-start | bytes 1572872 | tf_op jit(solution)/shard_map/ppermute | solution.py:239
  76.4 1.6 %collective-permute-start.23 = (bf16[1,512,512]{2,1,0:T(8,128)(2,1)S(1)}, bf16[1,512,512]{2,1,0:T(8,128)(2,1)S(1)}, u32[]{:S(2)}, u32[]{:S(2)}) collective-permute-start(bf16[1,512,512]{2,1,0:T(8,128)(2,1)S(1)} %shard_map.64.refs_0_), channel_id=1, source_target_pairs={{0,16},{1,9},{2,18},{3,11},{4,20},{5,13},{6,22},{7,15},{8,24},{9,1... | collective-permute-start | bytes 1572872 | tf_op jit(solution)/shard_map/ppermute | solution.py:239
  77.9 0.3 shard_map.63.refs_0_
  78.3 0.6 collective-permute-start.20
  78.8 3.0 %shard_map.55 = (s32[5193]{0:T(1024)S(4)}, f32[7]{0:T(128)S(4)}) custom-call(s32[3,12]{1,0:T(4,128)S(1)} %broadcast_add_fusion.own_ref, s32[3,12]{1,0:T(4,128)S(1)} %collective-permute-done.partner_ref, f32[1]{0:T(128)S(6)} %copy.40.occupancy, s32[3]{0:T(128)S(1)} %add_convert_fusion.sides, s32[3]{0:T(128)S(1)} %pad_add_fusion.place_ref), custom_call_target="tpu_custom_call" | custom-call | flops 1048576 | bytes 1048576 | tf_op jit(solution)/shard_map/pallas_call | solution.py:279
  82.1 0.3 shard_map.62.refs_0_
  82.5 1.6 %collective-permute-start.17 = (bf16[1,512,512]{2,1,0:T(8,128)(2,1)S(1)}, bf16[1,512,512]{2,1,0:T(8,128)(2,1)S(1)}, u32[]{:S(2)}, u32[]{:S(2)}) collective-permute-start(bf16[1,512,512]{2,1,0:T(8,128)(2,1)S(1)} %shard_map.62.refs_0_), channel_id=1, source_target_pairs={{0,16},{1,9},{2,18},{3,11},{4,20},{5,13},{6,22},{7,15},{8,24},{9,1... | collective-permute-start | bytes 1572872 | tf_op jit(solution)/shard_map/ppermute | solution.py:239
  84.0 3.3 %shard_map.66 = (bf16[13,512,512]{2,1,0:T(8,128)(2,1)S(1)}, f32[6,512,512]{2,1,0:T(8,128)S(1)}) custom-call(s32[5193]{0:T(1024)S(4)} %get-tuple-element.45.table, bf16[9,512,512]{2,1,0:T(8,128)(2,1)S(1)} %bitcast.12, bf16[1,512,512]{2,1,0:T(8,128)(2,1)S(1)} %shard_map.65.refs_0_, bf16[1,512,512]{2,1,0:T(8,128)(2,1)S(1)} %collective-permute-done.26.refs_1_), custom_call_target="tpu_custom_call" | custom-call | flops 2684354560 | bytes 1048576 | tf_op jit(solution)/shard_map/pallas_call | solution.py:279
  87.5 2.0 %collective-permute-start.5 = (bf16[1,256,512]{2,1,0:T(8,128)(2,1)S(1)}, bf16[1,256,512]{2,1,0:T(8,128)(2,1)S(1)}, u32[]{:S(2)}, u32[]{:S(2)}) collective-permute-start(bf16[1,256,512]{2,1,0:T(8,128)(2,1)S(1)} %shard_map.59.refs_2_), channel_id=1, source_target_pairs={{0,16},{1,9},{2,18},{3,11},{4,20},{5,13},{6,22},{7,15},{8,24},{9,1... | collective-permute-start | bytes 786440 | tf_op jit(solution)/shard_map/ppermute | solution.py:239
  89.9 2.9 %shard_map.67 = (bf16[13,512,512]{2,1,0:T(8,128)(2,1)S(1)}, f32[6,512,512]{2,1,0:T(8,128)S(1)}) custom-call(s32[5193]{0:T(1024)S(4)} %get-tuple-element.45.table, bf16[9,512,512]{2,1,0:T(8,128)(2,1)S(1)} %bitcast.12, bf16[1,512,512]{2,1,0:T(8,128)(2,1)S(1)} %shard_map.64.refs_0_, ...), custom_call_target="tpu_custom_call", output_to_operand_aliasing={{0}: (4, {}), {1}: (5, {})} | custom-call | flops 2684354560 | bytes 1048576 | tf_op jit(solution)/shard_map/pallas_call | solution.py:279
  92.8 2.3 %shard_map.68 = (bf16[13,512,512]{2,1,0:T(8,128)(2,1)S(1)}, f32[6,512,512]{2,1,0:T(8,128)S(1)}) custom-call(s32[5193]{0:T(1024)S(4)} %get-tuple-element.45.table, bf16[9,512,512]{2,1,0:T(8,128)(2,1)S(1)} %bitcast.12, bf16[1,512,512]{2,1,0:T(8,128)(2,1)S(1)} %shard_map.63.refs_0_, ...), custom_call_target="tpu_custom_call", output_to_operand_aliasing={{0}: (4, {}), {1}: (5, {})} | custom-call | flops 2684354560 | bytes 1048576 | tf_op jit(solution)/shard_map/pallas_call | solution.py:279
  95.1 1.7 %collective-permute-done.17.refs_1_ = bf16[1,512,512]{2,1,0:T(8,128)(2,1)S(1)} collective-permute-done((bf16[1,512,512]{2,1,0:T(8,128)(2,1)S(1)}, bf16[1,512,512]{2,1,0:T(8,128)(2,1)S(1)}, u32[]{:S(2)}, u32[]{:S(2)}) %collective-permute-start.17) | collective-permute-done | bytes 524320 | tf_op jit(solution)/shard_map/ppermute | solution.py:239
  96.8 3.1 %shard_map.69 = (bf16[13,512,512]{2,1,0:T(8,128)(2,1)S(1)}, f32[6,512,512]{2,1,0:T(8,128)S(1)}) custom-call(s32[5193]{0:T(1024)S(4)} %get-tuple-element.45.table, bf16[9,512,512]{2,1,0:T(8,128)(2,1)S(1)} %bitcast.12, bf16[1,512,512]{2,1,0:T(8,128)(2,1)S(1)} %shard_map.62.refs_0_, ...), custom_call_target="tpu_custom_call", output_to_operand_aliasing={{0}: (4, {}), {1}: (5, {})} | custom-call | flops 2684354560 | bytes 1048576 | tf_op jit(solution)/shard_map/pallas_call | solution.py:279
  99.9 8.2 %collective-permute-done.13.refs_1_ = bf16[1,512,512]{2,1,0:T(8,128)(2,1)S(1)} collective-permute-done((bf16[1,512,512]{2,1,0:T(8,128)(2,1)S(1)}, bf16[1,512,512]{2,1,0:T(8,128)(2,1)S(1)}, u32[]{:S(2)}, u32[]{:S(2)}) %collective-permute-start.13) | collective-permute-done | bytes 524320 | tf_op jit(solution)/shard_map/ppermute | solution.py:239
  108.1 5.3 %shard_map.70 = (bf16[13,512,512]{2,1,0:T(8,128)(2,1)S(1)}, f32[6,512,512]{2,1,0:T(8,128)S(1)}) custom-call(s32[5193]{0:T(1024)S(4)} %get-tuple-element.45.table, bf16[9,512,512]{2,1,0:T(8,128)(2,1)S(1)} %bitcast.12, bf16[1,512,512]{2,1,0:T(8,128)(2,1)S(1)} %shard_map.61.refs_0_, ...), custom_call_target="tpu_custom_call", output_to_operand_aliasing={{0}: (6, {}), {1}: (7, {})} | custom-call | flops 2684354560 | bytes 1048576 | tf_op jit(solution)/shard_map/pallas_call | solution.py:279
  113.4 0.9 shard_map.71
  114.3 0.9 shard_map.72
  115.3 2.0 %collective-permute-start.28 = (bf16[1,512,512]{2,1,0:T(8,128)(2,1)S(1)}, bf16[1,512,512]{2,1,0:T(8,128)(2,1)S(1)}, u32[]{:S(2)}, u32[]{:S(2)}) collective-permute-start(bf16[1,512,512]{2,1,0:T(8,128)(2,1)S(1)} %get-tuple-element.76), channel_id=1, source_target_pairs={{0,8},{1,17},{2,10},{3,19},{4,12},{5,21},{6,14},{7,23},{8,0},{9,25... | collective-permute-start | bytes 1572872 | tf_op jit(solution)/shard_map/ppermute | solution.py:239
  117.3 0.9 shard_map.73
  118.4 10.9 %shard_map.74 = (f32[6,512,512]{2,1,0:T(8,128)S(1)}, f32[3,1,2,512,512]{4,3,2,1,0:T(8,128)}) custom-call(s32[5193]{0:T(1024)S(4)} %get-tuple-element.45.table, s32[1]{0:T(128)} %bitcast.7.part_ref, bf16[9,512,512]{2,1,0:T(8,128)(2,1)S(1)} %bitcast.12, bf16[13,512,512]{2,1,0:T(8,128)(2,1)S(1)} %get-tuple-element.78.blocks, ...), custom_call_target="tpu_custom_call", output_to_operand_aliasing={{0}: (4, {})} | custom-call | flops 1048576 | bytes 1048576 | tf_op jit(solution)/shard_map/pallas_call | solution.py:279
  129.3 0.8 collective-permute-done.28.refs_0_
  130.1 1.4 %shard_map.75.refs_1_ = f32[3,1,2,512,512]{4,3,2,1,0:T(8,128)} custom-call(s32[1]{0:T(128)} %bitcast.part_ref, bf16[1,512,512]{2,1,0:T(8,128)(2,1)S(1)} %collective-permute-done.28.refs_0_, bf16[1,512,512]{2,1,0:T(8,128)(2,1)S(1)} %collective-permute-done.29.refs_1_, f32[3,1,2,512,512]{4,3,2,1,0:T(8,128)} %get-tuple-element.80.refs_2_), custom_call_target="tpu_custom_call", output_to_operand_aliasing={{}: (3, {})} | custom-call | flops 1048576 | bytes 1048576 | tf_op jit(solution)/shard_map/pallas_call | solution.py:279
  131.5 4.2 %collective-permute-done.27.refs_0_ = bf16[1,512,512]{2,1,0:T(8,128)(2,1)S(1)} collective-permute-done((bf16[1,512,512]{2,1,0:T(8,128)(2,1)S(1)}, bf16[1,512,512]{2,1,0:T(8,128)(2,1)S(1)}, u32[]{:S(2)}, u32[]{:S(2)}) %collective-permute-start.27) | collective-permute-done | bytes 524320 | tf_op jit(solution)/shard_map/ppermute | solution.py:239
  135.7 1.1 shard_map.76
  (50 shorter events, 2.1 us)
Async XLA Ops:
  0.9 0.7 copy-start
  1.5 10.8 %copy-start.1 = (s32[3]{0:T(128)S(1)}, s32[3]{0:T(128)}, u32[]{:S(2)}) copy-start(s32[3]{0:T(128)} %shift.1) | copy-start | bytes 40
  5.9 9.0 %copy-start.2 = (s32[3,12]{1,0:T(4,128)S(1)}, s32[3,12]{1,0:T(4,128)}, u32[]{:S(2)}) copy-start(s32[3,12]{1,0:T(4,128)} %param.6) | copy-start | bytes 436
  5.9 6.5 %collective-permute-start.1 = (bf16[6,512,512]{2,1,0:T(8,128)(2,1)S(1)}, bf16[6,512,512]{2,1,0:T(8,128)(2,1)S(1)}, u32[]{:S(2)}, u32[]{:S(2)}) collective-permute-start(bf16[6,512,512]{2,1,0:T(8,128)(2,1)S(1)} %get-tuple-element.49), channel_id=1, source_target_pairs={{0,1},{1,0},{2,3},{3,2},{4,5},{5,4},{6,7},{7,6},{8,9},{9,8},{10,11... | collective-permute-start | bytes 9437192 | tf_op jit(solution)/shard_map/ppermute | solution.py:239
  8.3 13.0 %collective-permute-start.25 = (bf16[1,512,512]{2,1,0:T(8,128)(2,1)S(1)}, bf16[1,512,512]{2,1,0:T(8,128)(2,1)S(1)}, u32[]{:S(2)}, u32[]{:S(2)}) collective-permute-start(bf16[1,512,512]{2,1,0:T(8,128)(2,1)S(1)} %shard_map.57.refs_0_), channel_id=1, source_target_pairs={{0,1},{1,3},{2,0},{3,5},{4,2},{5,7},{6,4},{7,6},{8,9},{9,11},{10,8... | collective-permute-start | bytes 1572872 | tf_op jit(solution)/shard_map/ppermute | solution.py:239
  8.3 15.6 %collective-permute-start.22 = (bf16[1,512,512]{2,1,0:T(8,128)(2,1)S(1)}, bf16[1,512,512]{2,1,0:T(8,128)(2,1)S(1)}, u32[]{:S(2)}, u32[]{:S(2)}) collective-permute-start(bf16[1,512,512]{2,1,0:T(8,128)(2,1)S(1)} %get-tuple-element.50.refs_1_), channel_id=1, source_target_pairs={{0,1},{1,3},{2,0},{3,5},{4,2},{5,7},{6,4},{7,6},{8,9},{9,11},{10,8... | collective-permute-start | bytes 1572872 | tf_op jit(solution)/shard_map/ppermute | solution.py:239
  11.1 23.8 %collective-permute-start.19 = (bf16[1,512,512]{2,1,0:T(8,128)(2,1)S(1)}, bf16[1,512,512]{2,1,0:T(8,128)(2,1)S(1)}, u32[]{:S(2)}, u32[]{:S(2)}) collective-permute-start(bf16[1,512,512]{2,1,0:T(8,128)(2,1)S(1)} %get-tuple-element.51.refs_2_), channel_id=1, source_target_pairs={{0,1},{1,3},{2,0},{3,5},{4,2},{5,7},{6,4},{7,6},{8,9},{9,11},{10,8... | collective-permute-start | bytes 1572872 | tf_op jit(solution)/shard_map/ppermute | solution.py:239
  12.4 71.7 %slice-start = ((s8[4718592]{0:T(1024)(128)(4,1)}), s8[4194304]{0:T(1024)(128)(4,1)S(1)}, s32[]{:S(2)}) async-start(s8[4718592]{0:T(1024)(128)(4,1)} %bitcast.11), calls=%async_computation | async-start | bytes 8388608
  12.7 24.2 %collective-permute-start.6 = (bf16[1,256,512]{2,1,0:T(8,128)(2,1)S(1)}, bf16[1,256,512]{2,1,0:T(8,128)(2,1)S(1)}, u32[]{:S(2)}, u32[]{:S(2)}) collective-permute-start(bf16[1,256,512]{2,1,0:T(8,128)(2,1)S(1)} %get-tuple-element.54), channel_id=1, source_target_pairs={{0,8},{1,17},{2,10},{3,19},{4,12},{5,21},{6,14},{7,23},{8,0},{9,25... | collective-permute-start | bytes 786440 | tf_op jit(solution)/shard_map/ppermute | solution.py:239
  15.0 4.3 %collective-permute-start = (s32[3,12]{1,0:T(4,128)S(1)}, s32[3,12]{1,0:T(4,128)S(1)}, u32[]{:S(2)}, u32[]{:S(2)}) collective-permute-start(s32[3,12]{1,0:T(4,128)S(1)} %broadcast_add_fusion.own_ref), channel_id=1, source_target_pairs={{0,8},{1,17},{2,10},{3,19},{4,12},{5,21},{6,14},{7,23},{8,0},{9,25... | collective-permute-start | bytes 440 | tf_op jit(solution)/shard_map/ppermute | solution.py:239
  19.3 19.2 %collective-permute-start.2 = (bf16[1,256,512]{2,1,0:T(8,128)(2,1)S(1)}, bf16[1,256,512]{2,1,0:T(8,128)(2,1)S(1)}, u32[]{:S(2)}, u32[]{:S(2)}) collective-permute-start(bf16[1,256,512]{2,1,0:T(8,128)(2,1)S(1)} %get-tuple-element.53), channel_id=1, source_target_pairs={{0,8},{1,17},{2,10},{3,19},{4,12},{5,21},{6,14},{7,23},{8,0},{9,25... | collective-permute-start | bytes 786440 | tf_op jit(solution)/shard_map/ppermute | solution.py:239
  21.3 18.7 %collective-permute-start.24 = (bf16[1,512,512]{2,1,0:T(8,128)(2,1)S(1)}, bf16[1,512,512]{2,1,0:T(8,128)(2,1)S(1)}, u32[]{:S(2)}, u32[]{:S(2)}) collective-permute-start(bf16[1,512,512]{2,1,0:T(8,128)(2,1)S(1)} %get-tuple-element.60.chosen), channel_id=1, source_target_pairs={{0,2},{1,0},{2,4},{3,1},{4,6},{5,3},{6,7},{7,5},{8,10},{9,8},{10,1... | collective-permute-start | bytes 1572872 | tf_op jit(solution)/shard_map/ppermute | solution.py:239
  23.8 16.2 %collective-permute-start.14 = (bf16[1,512,512]{2,1,0:T(8,128)(2,1)S(1)}, bf16[1,512,512]{2,1,0:T(8,128)(2,1)S(1)}, u32[]{:S(2)}, u32[]{:S(2)}) collective-permute-start(bf16[1,512,512]{2,1,0:T(8,128)(2,1)S(1)} %get-tuple-element.56), channel_id=1, source_target_pairs={{0,8},{1,17},{2,10},{3,19},{4,12},{5,21},{6,14},{7,23},{8,0},{9,25... | collective-permute-start | bytes 1572872 | tf_op jit(solution)/shard_map/ppermute | solution.py:239
  34.9 8.7 %collective-permute-start.21 = (bf16[1,512,512]{2,1,0:T(8,128)(2,1)S(1)}, bf16[1,512,512]{2,1,0:T(8,128)(2,1)S(1)}, u32[]{:S(2)}, u32[]{:S(2)}) collective-permute-start(bf16[1,512,512]{2,1,0:T(8,128)(2,1)S(1)} %get-tuple-element.59.chosen), channel_id=1, source_target_pairs={{0,2},{1,0},{2,4},{3,1},{4,6},{5,3},{6,7},{7,5},{8,10},{9,8},{10,1... | collective-permute-start | bytes 1572872 | tf_op jit(solution)/shard_map/ppermute | solution.py:239
  36.9 17.8 %collective-permute-start.18 = (bf16[1,512,512]{2,1,0:T(8,128)(2,1)S(1)}, bf16[1,512,512]{2,1,0:T(8,128)(2,1)S(1)}, u32[]{:S(2)}, u32[]{:S(2)}) collective-permute-start(bf16[1,512,512]{2,1,0:T(8,128)(2,1)S(1)} %get-tuple-element.58.chosen), channel_id=1, source_target_pairs={{0,2},{1,0},{2,4},{3,1},{4,6},{5,3},{6,7},{7,5},{8,10},{9,8},{10,1... | collective-permute-start | bytes 1572872 | tf_op jit(solution)/shard_map/ppermute | solution.py:239
  38.5 16.2 %collective-permute-start.10 = (bf16[1,512,512]{2,1,0:T(8,128)(2,1)S(1)}, bf16[1,512,512]{2,1,0:T(8,128)(2,1)S(1)}, u32[]{:S(2)}, u32[]{:S(2)}) collective-permute-start(bf16[1,512,512]{2,1,0:T(8,128)(2,1)S(1)} %get-tuple-element.55), channel_id=1, source_target_pairs={{0,8},{1,17},{2,10},{3,19},{4,12},{5,21},{6,14},{7,23},{8,0},{9,25... | collective-permute-start | bytes 1572872 | tf_op jit(solution)/shard_map/ppermute | solution.py:239
  40.0 20.4 %collective-permute-start.7 = (bf16[1,256,512]{2,1,0:T(8,128)(2,1)S(1)}, bf16[1,256,512]{2,1,0:T(8,128)(2,1)S(1)}, u32[]{:S(2)}, u32[]{:S(2)}) collective-permute-start(bf16[1,256,512]{2,1,0:T(8,128)(2,1)S(1)} %collective-permute-done.6.chosen), channel_id=1, source_target_pairs={{0,2},{1,0},{2,4},{3,1},{4,6},{5,3},{6,7},{7,5},{8,10},{9,8},{10,1... | collective-permute-start | bytes 786440 | tf_op jit(solution)/shard_map/ppermute | solution.py:239
  40.0 36.3 %collective-permute-start.15 = (bf16[1,512,512]{2,1,0:T(8,128)(2,1)S(1)}, bf16[1,512,512]{2,1,0:T(8,128)(2,1)S(1)}, u32[]{:S(2)}, u32[]{:S(2)}) collective-permute-start(bf16[1,512,512]{2,1,0:T(8,128)(2,1)S(1)} %collective-permute-done.14.chosen), channel_id=1, source_target_pairs={{0,2},{1,0},{2,4},{3,1},{4,6},{5,3},{6,7},{7,5},{8,10},{9,8},{10,1... | collective-permute-start | bytes 1572872 | tf_op jit(solution)/shard_map/ppermute | solution.py:239
  43.6 17.0 %collective-permute-start.8 = (bf16[1,256,512]{2,1,0:T(8,128)(2,1)S(1)}, bf16[1,256,512]{2,1,0:T(8,128)(2,1)S(1)}, u32[]{:S(2)}, u32[]{:S(2)}) collective-permute-start(bf16[1,256,512]{2,1,0:T(8,128)(2,1)S(1)} %collective-permute-done.6.chosen), channel_id=1, source_target_pairs={{0,1},{1,3},{2,0},{3,5},{4,2},{5,7},{6,4},{7,6},{8,9},{9,11},{10,8... | collective-permute-start | bytes 786440 | tf_op jit(solution)/shard_map/ppermute | solution.py:239
  54.7 23.6 %collective-permute-start.16 = (bf16[1,512,512]{2,1,0:T(8,128)(2,1)S(1)}, bf16[1,512,512]{2,1,0:T(8,128)(2,1)S(1)}, u32[]{:S(2)}, u32[]{:S(2)}) collective-permute-start(bf16[1,512,512]{2,1,0:T(8,128)(2,1)S(1)} %collective-permute-done.14.chosen), channel_id=1, source_target_pairs={{0,1},{1,3},{2,0},{3,5},{4,2},{5,7},{6,4},{7,6},{8,9},{9,11},{10,8... | collective-permute-start | bytes 1572872 | tf_op jit(solution)/shard_map/ppermute | solution.py:239
  54.7 17.0 %collective-permute-start.3 = (bf16[1,256,512]{2,1,0:T(8,128)(2,1)S(1)}, bf16[1,256,512]{2,1,0:T(8,128)(2,1)S(1)}, u32[]{:S(2)}, u32[]{:S(2)}) collective-permute-start(bf16[1,256,512]{2,1,0:T(8,128)(2,1)S(1)} %collective-permute-done.2.chosen), channel_id=1, source_target_pairs={{0,2},{1,0},{2,4},{3,1},{4,6},{5,3},{6,7},{7,5},{8,10},{9,8},{10,1... | collective-permute-start | bytes 786440 | tf_op jit(solution)/shard_map/ppermute | solution.py:239
  60.3 15.7 %collective-permute-start.4 = (bf16[1,256,512]{2,1,0:T(8,128)(2,1)S(1)}, bf16[1,256,512]{2,1,0:T(8,128)(2,1)S(1)}, u32[]{:S(2)}, u32[]{:S(2)}) collective-permute-start(bf16[1,256,512]{2,1,0:T(8,128)(2,1)S(1)} %collective-permute-done.2.chosen), channel_id=1, source_target_pairs={{0,1},{1,3},{2,0},{3,5},{4,2},{5,7},{6,4},{7,6},{8,9},{9,11},{10,8... | collective-permute-start | bytes 786440 | tf_op jit(solution)/shard_map/ppermute | solution.py:239
  60.3 23.7 %slice-start.1 = ((s8[4718592]{0:T(1024)(128)(4,1)}), s8[524288]{0:T(1024)(128)(4,1)S(1)}, s32[]{:S(2)}) async-start(s8[4718592]{0:T(1024)(128)(4,1)} %bitcast.11), calls=%async_computation.1 | async-start | bytes 1048576
  60.6 21.8 %collective-permute-start.26 = (bf16[1,512,512]{2,1,0:T(8,128)(2,1)S(1)}, bf16[1,512,512]{2,1,0:T(8,128)(2,1)S(1)}, u32[]{:S(2)}, u32[]{:S(2)}) collective-permute-start(bf16[1,512,512]{2,1,0:T(8,128)(2,1)S(1)} %shard_map.65.refs_0_), channel_id=1, source_target_pairs={{0,16},{1,9},{2,18},{3,11},{4,20},{5,13},{6,22},{7,15},{8,24},{9,1... | collective-permute-start | bytes 1572872 | tf_op jit(solution)/shard_map/ppermute | solution.py:239
  71.7 15.7 %collective-permute-start.11 = (bf16[1,512,512]{2,1,0:T(8,128)(2,1)S(1)}, bf16[1,512,512]{2,1,0:T(8,128)(2,1)S(1)}, u32[]{:S(2)}, u32[]{:S(2)}) collective-permute-start(bf16[1,512,512]{2,1,0:T(8,128)(2,1)S(1)} %collective-permute-done.10.chosen), channel_id=1, source_target_pairs={{0,2},{1,0},{2,4},{3,1},{4,6},{5,3},{6,7},{7,5},{8,10},{9,8},{10,1... | collective-permute-start | bytes 1572872 | tf_op jit(solution)/shard_map/ppermute | solution.py:239
  76.0 11.4 %collective-permute-start.12 = (bf16[1,512,512]{2,1,0:T(8,128)(2,1)S(1)}, bf16[1,512,512]{2,1,0:T(8,128)(2,1)S(1)}, u32[]{:S(2)}, u32[]{:S(2)}) collective-permute-start(bf16[1,512,512]{2,1,0:T(8,128)(2,1)S(1)} %collective-permute-done.10.chosen), channel_id=1, source_target_pairs={{0,1},{1,3},{2,0},{3,5},{4,2},{5,7},{6,4},{7,6},{8,9},{9,11},{10,8... | collective-permute-start | bytes 1572872 | tf_op jit(solution)/shard_map/ppermute | solution.py:239
  76.4 13.4 %collective-permute-start.23 = (bf16[1,512,512]{2,1,0:T(8,128)(2,1)S(1)}, bf16[1,512,512]{2,1,0:T(8,128)(2,1)S(1)}, u32[]{:S(2)}, u32[]{:S(2)}) collective-permute-start(bf16[1,512,512]{2,1,0:T(8,128)(2,1)S(1)} %shard_map.64.refs_0_), channel_id=1, source_target_pairs={{0,16},{1,9},{2,18},{3,11},{4,20},{5,13},{6,22},{7,15},{8,24},{9,1... | collective-permute-start | bytes 1572872 | tf_op jit(solution)/shard_map/ppermute | solution.py:239
  78.3 14.6 %collective-permute-start.20 = (bf16[1,512,512]{2,1,0:T(8,128)(2,1)S(1)}, bf16[1,512,512]{2,1,0:T(8,128)(2,1)S(1)}, u32[]{:S(2)}, u32[]{:S(2)}) collective-permute-start(bf16[1,512,512]{2,1,0:T(8,128)(2,1)S(1)} %shard_map.63.refs_0_), channel_id=1, source_target_pairs={{0,16},{1,9},{2,18},{3,11},{4,20},{5,13},{6,22},{7,15},{8,24},{9,1... | collective-permute-start | bytes 1572872 | tf_op jit(solution)/shard_map/ppermute | solution.py:239
  82.5 14.4 %collective-permute-start.17 = (bf16[1,512,512]{2,1,0:T(8,128)(2,1)S(1)}, bf16[1,512,512]{2,1,0:T(8,128)(2,1)S(1)}, u32[]{:S(2)}, u32[]{:S(2)}) collective-permute-start(bf16[1,512,512]{2,1,0:T(8,128)(2,1)S(1)} %shard_map.62.refs_0_), channel_id=1, source_target_pairs={{0,16},{1,9},{2,18},{3,11},{4,20},{5,13},{6,22},{7,15},{8,24},{9,1... | collective-permute-start | bytes 1572872 | tf_op jit(solution)/shard_map/ppermute | solution.py:239
  87.4 26.0 %collective-permute-start.9 = (bf16[1,256,512]{2,1,0:T(8,128)(2,1)S(1)}, bf16[1,256,512]{2,1,0:T(8,128)(2,1)S(1)}, u32[]{:S(2)}, u32[]{:S(2)}) collective-permute-start(bf16[1,256,512]{2,1,0:T(8,128)(2,1)S(1)} %shard_map.60.refs_3_), channel_id=1, source_target_pairs={{0,16},{1,9},{2,18},{3,11},{4,20},{5,13},{6,22},{7,15},{8,24},{9,1... | collective-permute-start | bytes 786440 | tf_op jit(solution)/shard_map/ppermute | solution.py:239
  87.5 25.9 %collective-permute-start.5 = (bf16[1,256,512]{2,1,0:T(8,128)(2,1)S(1)}, bf16[1,256,512]{2,1,0:T(8,128)(2,1)S(1)}, u32[]{:S(2)}, u32[]{:S(2)}) collective-permute-start(bf16[1,256,512]{2,1,0:T(8,128)(2,1)S(1)} %shard_map.59.refs_2_), channel_id=1, source_target_pairs={{0,16},{1,9},{2,18},{3,11},{4,20},{5,13},{6,22},{7,15},{8,24},{9,1... | collective-permute-start | bytes 786440 | tf_op jit(solution)/shard_map/ppermute | solution.py:239
  89.8 18.3 %collective-permute-start.13 = (bf16[1,512,512]{2,1,0:T(8,128)(2,1)S(1)}, bf16[1,512,512]{2,1,0:T(8,128)(2,1)S(1)}, u32[]{:S(2)}, u32[]{:S(2)}) collective-permute-start(bf16[1,512,512]{2,1,0:T(8,128)(2,1)S(1)} %shard_map.61.refs_0_), channel_id=1, source_target_pairs={{0,16},{1,9},{2,18},{3,11},{4,20},{5,13},{6,22},{7,15},{8,24},{9,1... | collective-permute-start | bytes 1572872 | tf_op jit(solution)/shard_map/ppermute | solution.py:239
  115.2 14.1 %collective-permute-start.29 = (bf16[1,512,512]{2,1,0:T(8,128)(2,1)S(1)}, bf16[1,512,512]{2,1,0:T(8,128)(2,1)S(1)}, u32[]{:S(2)}, u32[]{:S(2)}) collective-permute-start(bf16[1,512,512]{2,1,0:T(8,128)(2,1)S(1)} %get-tuple-element.77), channel_id=1, source_target_pairs={{0,8},{1,17},{2,10},{3,19},{4,12},{5,21},{6,14},{7,23},{8,0},{9,25... | collective-permute-start | bytes 1572872 | tf_op jit(solution)/shard_map/ppermute | solution.py:239
  115.3 14.8 %collective-permute-start.28 = (bf16[1,512,512]{2,1,0:T(8,128)(2,1)S(1)}, bf16[1,512,512]{2,1,0:T(8,128)(2,1)S(1)}, u32[]{:S(2)}, u32[]{:S(2)}) collective-permute-start(bf16[1,512,512]{2,1,0:T(8,128)(2,1)S(1)} %get-tuple-element.76), channel_id=1, source_target_pairs={{0,8},{1,17},{2,10},{3,19},{4,12},{5,21},{6,14},{7,23},{8,0},{9,25... | collective-permute-start | bytes 1572872 | tf_op jit(solution)/shard_map/ppermute | solution.py:239
  118.2 17.5 %collective-permute-start.27 = (bf16[1,512,512]{2,1,0:T(8,128)(2,1)S(1)}, bf16[1,512,512]{2,1,0:T(8,128)(2,1)S(1)}, u32[]{:S(2)}, u32[]{:S(2)}) collective-permute-start(bf16[1,512,512]{2,1,0:T(8,128)(2,1)S(1)} %get-tuple-element.75), channel_id=1, source_target_pairs={{0,8},{1,17},{2,10},{3,19},{4,12},{5,21},{6,14},{7,23},{8,0},{9,25... | collective-permute-start | bytes 1572872 | tf_op jit(solution)/shard_map/ppermute | solution.py:239
